TPU v7x, 512 devices: a whole 4x4x16 slice. The times are simulated.
512 devices in a mesh: prow: 16 (over y, z_hi, core), pcol: 32 (over x, z_lo).
Axes of the slice: x: 4, y: 4, z: 16 (z_hi: 2, z_lo: 8; z = z_hi * 8 + z_lo), core: 2. Of those that a mesh axis runs over, the one named last changes fastest.
Arguments:
- tiles: bfloat16 [16, 32, 16, 256, 256], P('prow', 'pcol'), may hold values from -6 to 6
- tile_ids: int32 [16, 32, 16], P('prow', 'pcol'), may hold values from 0 to 127, as said below
- counts: int32 [16, 32], P('prow', 'pcol'), may hold values from 1 to 16, as said below
- pivots: int32 [256], replicated, may hold values from 0 to 65535, as said below
- l_inverse: bfloat16 [256, 256], P(None, 'pcol'), may hold values from -1 to 1, as said below
- u_inverse: bfloat16 [256, 256], P('prow'), may hold values from -0.125 to 0.5, as said below
Outputs:
- factored: bfloat16 [16, 32, 16, 256, 256], P('prow', 'pcol')
Inputs may be any that keep to these rules, and one draw needn't show every extreme that they name: Live slot s of device (p, q) holds local tile row tile_ids[p, q, s] // 8 and local tile column tile_ids[p, q, s] % 8; live codes of one device are distinct, padded slots hold arbitrary codes. Let R be the tile rows I >= 1 with tile (I, 0) held and C the tile columns J >= 1 with tile (0, J) held. Tile (0, 0) is held; on each prow index R takes the last one to 3 local tile rows, on each pcol index C takes the last one to 3 local tile columns, and both most counts are reached on some index. Every tile whose row is 0 or in R and whose column is 0 or in C is held; no other held tile lies in tile row 0, a tile row of R, or tile column 0. `counts`: some device has 16 live slots. Row r of tile row 0 and row pivots[r] change places; pivots[r] is r or a row of a tile row of R, and the values that differ from their r are distinct. `l_inverse`: lower triangular with unit diagonal. `u_inverse`: upper triangular with a positive diagonal.
All inputs are finite; a program needn't handle non-finite values.
Results may differ from a plain program's by a relative error of at most 0.0056.
Values may be sent and summed in bfloat16 or wider, within the bound.
A program may use at most 64 MiB of HBM per device.

v0:
```python
import jax
import jax.numpy as jnp
from jax import lax
from jax.sharding import Mesh
from jax.sharding import PartitionSpec as P

TILE_SIDE = 256
LOCAL_ROWS = 16
TILE_SLOTS = 16
LOWER_MOST = 3
UPPER_MOST = 3
HALF_WORK = 4
PCOL = ("pcol_0", "pcol_1")


def laid_out(parts, dim):
    parts = jnp.moveaxis(parts, 0, dim)
    lengths = parts.shape
    return parts.reshape(*lengths[:dim], lengths[dim] * lengths[dim + 1], *lengths[dim + 2 :])


def from_everyone(shard, axis):
    devices = lax.axis_size(axis)
    return lax.all_to_all(
        jnp.broadcast_to(shard[None], (devices, *shard.shape)), axis, 0, 0, tiled=True
    )


def gather_directly(shard, axis, dim):
    return laid_out(from_everyone(shard, axis), dim)


def spread(shard, axes, root):
    shard = jnp.where(lax.axis_index(axes) == root, shard, jnp.zeros_like(shard))
    for axis in axes:
        shard = lax.psum(shard, axis)
    return shard


def from_partner(block, axis, bit):
    count = lax.axis_size(axis)
    route = []
    for low in range(count):
        high = low | 1 << bit
        if high != low and high < count:
            route += [(low, high), (high, low)]
    return lax.ppermute(block, axis, route)


def pick_rows(tile, rows):
    return tile[rows]


def body(tiles, tile_ids, counts, pivots, l_inverse, u_inverse):
    row_count = lax.axis_size("prow")
    col_count = lax.axis_size(PCOL)
    my_row = lax.axis_index("prow")
    my_col = lax.axis_index(PCOL)
    grid_cols = LOCAL_ROWS * row_count // col_count
    total_rows = LOCAL_ROWS * row_count * TILE_SIDE
    local = tiles[0, 0]
    codes = tile_ids[0, 0]
    slot_range = jnp.arange(TILE_SLOTS, dtype=jnp.int32)
    alive = slot_range < counts[0, 0]
    loc_row = codes // grid_cols
    loc_col = codes % grid_cols
    glob_row = my_row + row_count * loc_row
    glob_col = my_col + col_count * loc_col
    col_range = jnp.arange(grid_cols, dtype=jnp.int32)
    upper_inv = lax.all_gather(u_inverse, "prow", axis=0, tiled=True)
    lower_inv = gather_directly(l_inverse, PCOL, 1)
    source_tile = pivots // TILE_SIDE
    source_row = pivots % TILE_SIDE
    gathered = local[:, source_row, :]
    owned = (source_tile[None, :] == glob_row[:, None]) & alive[:, None]
    contrib = jnp.where(owned[:, :, None], gathered, jnp.zeros_like(gathered))
    col_hot = ((loc_col[:, None] == col_range[None, :]) & alive[:, None]).astype(jnp.bfloat16)
    top_flag = (glob_row == 0).astype(jnp.bfloat16)
    top_hot = col_hot * top_flag[:, None]
    flag_part = jnp.sum(
        top_hot.astype(jnp.float32) * (glob_col >= 1).astype(jnp.float32)[:, None], axis=0
    )
    list_size = UPPER_MOST + 1
    rows_used = (glob_row == 0) | jnp.any(owned, axis=1)
    col_mask = jnp.any(
        (loc_col[:, None] == col_range[None, :]) & (alive & rows_used)[:, None], axis=0
    )
    listed = jnp.argsort(jnp.where(col_mask, 0, 1), stable=True)[:list_size]
    list_valid = col_mask[listed]
    list_hot = (
        (loc_col[:, None] == listed[None, :]) & list_valid[None, :] & alive[:, None]
    ).astype(jnp.bfloat16)
    new_part = jnp.einsum("sk,srb->krb", list_hot, contrib, preferred_element_type=jnp.float32)
    old_part = jnp.einsum(
        "sk,srb->krb", list_hot * top_flag[:, None], local, preferred_element_type=jnp.float32
    )
    id_part = jnp.where(list_valid & (my_row == 0), listed + 1, 0).astype(jnp.float32)
    new_sum, old_sum, flag_sum, id_sum = (
        lax.psum(new_part.astype(jnp.bfloat16), "prow").astype(jnp.float32),
        lax.psum(old_part.astype(jnp.bfloat16), "prow").astype(jnp.float32),
        lax.psum(flag_part.astype(jnp.bfloat16), "prow").astype(jnp.float32),
        lax.psum(id_part.astype(jnp.bfloat16), "prow").astype(jnp.float32),
    )
    list_ids = (id_sum + 0.5).astype(jnp.int32) - 1
    back_hot = ((list_ids[:, None] == col_range[None, :]) & (id_sum > 0.5)[:, None]).astype(
        jnp.bfloat16
    )
    new_top = jnp.einsum(
        "kj,krb->jrb", back_hot, new_sum.astype(jnp.bfloat16), preferred_element_type=jnp.float32
    ).astype(jnp.bfloat16)
    old_top = jnp.einsum(
        "kj,krb->jrb", back_hot, old_sum.astype(jnp.bfloat16), preferred_element_type=jnp.float32
    ).astype(jnp.bfloat16)
    anchor_top = (
        jnp.full((total_rows,), -1, jnp.int32)
        .at[pivots]
        .set(jnp.arange(TILE_SIDE, dtype=jnp.int32))
    )
    row_index = glob_row[:, None] * TILE_SIDE + jnp.arange(TILE_SIDE, dtype=jnp.int32)[None, :]
    anchor = anchor_top[row_index]
    moved = (anchor >= 0) & (glob_row >= 1)[:, None]
    from_top = jax.vmap(pick_rows)(old_top[loc_col], jnp.maximum(anchor, 0))
    swapped = jnp.where(moved[:, :, None], from_top, local)
    primed = jnp.where((glob_row == 0)[:, None, None], new_top[loc_col], swapped)
    panel_mask = alive & (glob_col == 0) & (glob_row >= 1)
    panel_slots = jnp.argsort(jnp.where(panel_mask, 0, 1), stable=True)[:LOWER_MOST]
    panel_valid = panel_mask[panel_slots]
    lower_full = jnp.einsum(
        "kab,bc->kac", primed[panel_slots], upper_inv, preferred_element_type=jnp.float32
    )
    lower_list = jnp.where(panel_valid[:, None, None], lower_full, 0.0).astype(jnp.bfloat16)
    lower_rows = jnp.where(panel_valid, loc_row[panel_slots], -1)
    got_list, got_rows = (spread(lower_list, PCOL, 0), spread(lower_rows, PCOL, 0))
    row_match = got_rows[None, :] == loc_row[:, None]
    lower_pick = jnp.sum(
        jnp.where(row_match, jnp.arange(LOWER_MOST, dtype=jnp.int32)[None, :], 0), axis=1
    )
    lower_present = jnp.any(row_match, axis=1)
    column_flags = flag_sum > 0.5
    column_order = jnp.argsort(jnp.where(column_flags, 0, 1), stable=True)[:UPPER_MOST]
    upper_valid = column_flags[column_order]
    upper_full = jnp.einsum(
        "ab,kbc->kac", lower_inv, new_top[column_order], preferred_element_type=jnp.float32
    )
    upper_list = jnp.where(upper_valid[:, None, None], upper_full, 0.0).astype(jnp.bfloat16)
    upper_ids = jnp.where(upper_valid, column_order, -1)
    col_match = upper_ids[None, :] == loc_col[:, None]
    upper_pick = jnp.sum(
        jnp.where(col_match, jnp.arange(UPPER_MOST, dtype=jnp.int32)[None, :], 0), axis=1
    )
    upper_present = jnp.any(col_match, axis=1)
    result = jnp.where(alive[:, None, None], primed, jnp.zeros_like(primed))
    upper_mask = alive & (glob_row == 0) & (glob_col >= 1)
    result = jnp.where(upper_mask[:, None, None], upper_list[upper_pick], result)
    result = result.at[panel_slots].set(
        jnp.where(panel_valid[:, None, None], lower_list, result[panel_slots])
    )
    needs = alive & (glob_row >= 1) & (glob_col >= 1) & lower_present & upper_present
    order = jnp.argsort(jnp.where(needs, 0, 1), stable=True)
    needed = jnp.sum(needs.astype(jnp.int32))

    def trailing(current, lower_tile, upper_index):
        product = jnp.dot(lower_tile, upper_list[upper_index], preferred_element_type=jnp.float32)
        return (current.astype(jnp.float32) - product).astype(jnp.bfloat16)

    half_index = jnp.arange(HALF_WORK, dtype=jnp.int32)
    odd_slots = order[2 * half_index + 1]
    sent_count = needed // 2
    partner_bit = row_count.bit_length() - 2
    got_tiles, got_lower, got_pick, got_count = from_partner(
        (primed[odd_slots], got_list[lower_pick[odd_slots]], upper_pick[odd_slots], sent_count),
        "prow",
        partner_bit,
    )

    def remote_step(position, held):
        value = trailing(got_tiles[position], got_lower[position], got_pick[position])
        return held.at[position].set(value)

    finished = lax.fori_loop(0, got_count, remote_step, jnp.zeros_like(got_tiles))
    returned = from_partner(finished, "prow", partner_bit)

    def even_step(position, held):
        slot = order[2 * position]
        value = trailing(primed[slot], got_list[lower_pick[slot]], upper_pick[slot])
        return held.at[slot].set(value)

    result = lax.fori_loop(0, (needed + 1) // 2, even_step, result)
    sent_live = half_index < sent_count
    result = result.at[odd_slots].set(
        jnp.where(sent_live[:, None, None], returned, result[odd_slots])
    )
    return result[None, None]


def solution(mesh):
    torus = Mesh(mesh.devices.reshape(mesh.shape["prow"], 4, 8), ("prow", "pcol_0", "pcol_1"))
    placed = (
        P("prow", PCOL, None, None, None),
        P("prow", PCOL, None),
        P("prow", PCOL),
        P(),
        P(None, PCOL),
        P("prow", None),
    )
    return jax.shard_map(
        body,
        mesh=torus,
        in_specs=placed,
        out_specs=P("prow", PCOL, None, None, None),
        check_vma=False,
    )
```

profile of v0, /device:TPU:24, one launch (start us, length us, event | category | flops | bytes accessed | tf_op | source)
XLA Modules:
  0.0 688.9 jit_solution(12001899202512432619)
XLA Ops:
  6.5 1.3 broadcast_in_dim.201
  7.9 15.4 %all-to-all-start = ((bf16[32,256,8]{1,2,0:T(8,128)(2,1)}), bf16[32,256,8]{1,2,0:T(8,128)(2,1)S(1)}, u32[]{:S(2)}, u32[]{:S(2)}) async-start(bf16[32,256,8]{1,2,0:T(8,128)(2,1)} %broadcast_in_dim.201), calls=%async_computation | async-start | bytes 262144 | tf_op jit(solution)/shard_map/all_to_all | solution.py:24
  26.1 1.0 sort.63
  27.8 4.1 copy.83
  31.9 3.8 gather_fusion.2
  35.8 2.1 convolution_convert_fusion.2
  37.9 2.2 fusion.20
  40.3 64.7 %all-reduce = (bf16[4]{0:T(256)(128)(2,1)S(1)}, bf16[8]{0:T(256)(128)(2,1)S(1)}) all-reduce(bf16[4]{0:T(256)(128)(2,1)S(1)} %get-tuple-element.249, bf16[8]{0:T(256)(128)(2,1)S(1)} %multiply_reduce_fusion), channel_id=1, replica_groups=mesh['prow'=16,'pcol_0'=4,'pcol_1'=8] {'prow'}, use_global_device_ids=true, to_apply=%region_6.7 | all-reduce | flops 12 | bytes 48 | tf_op jit(solution)/shard_map/psum | solution.py:102
  105.0 1.0 sort.62
  106.7 1.3 sort.64
  109.4 9.3 %psum.60 = s32[3]{0:T(128)S(1)} all-reduce(s32[3]{0:T(128)S(1)} %broadcast_select_fusion.3), channel_id=1, replica_groups=mesh['prow'=16,'pcol_0'=4,'pcol_1'=8] {'pcol_0'}, use_global_device_ids=true, to_apply=%region_13.14 | all-reduce | flops 3 | bytes 24 | tf_op jit(solution)/shard_map/psum | solution.py:36
  118.7 16.9 %psum.61 = s32[3]{0:T(128)S(1)} all-reduce(s32[3]{0:T(128)S(1)} %psum.60), channel_id=1, replica_groups=mesh['prow'=16,'pcol_0'=4,'pcol_1'=8] {'pcol_1'}, use_global_device_ids=true, to_apply=%region_14.15 | all-reduce | flops 3 | bytes 24 | tf_op jit(solution)/shard_map/psum | solution.py:36
  136.4 1.5 scatter_custom_fusion
  137.9 23.0 %gather_fusion.6 = s32[4096]{0:T(1024)S(1)} fusion(s32[65536]{0:T(1024)S(1)} %scatter_custom_fusion, s32[4096]{0:T(1024)S(1)} %broadcast_clamp_fusion), kind=kCustom, calls=%fused_computation.6 | custom fusion | bytes 49152 | tf_op jit(solution)/shard_map/gather | solution.py:120
  161.3 36.9 %all_gather.3 = bf16[256,256]{1,0:T(8,128)(2,1)S(1)} all-gather(bf16[16,256]{1,0:T(8,128)(2,1)S(1)} %copy-done.9), channel_id=1, replica_groups=mesh['prow'=16,'pcol_0'=4,'pcol_1'=8] {'prow'}, dimensions={0}, use_global_device_ids=true | all-gather | bytes 139264 | tf_op jit(solution)/shard_map/all_gather | solution.py:70
  198.3 115.9 %all-reduce.10.cloned.1.call-done = (bf16[4,256,256]{2,0,1:T(4,128)(2,1)}, bf16[4,256,256]{2,0,1:T(4,128)(2,1)}) async-done(((bf16[4,256,256]{2,0,1:T(4,128)(2,1)}, bf16[4,256,256]{2,0,1:T(4,128)(2,1)}), (bf16[4,256,256]{2,0,1:T(4,128)(2,1)}, bf16[4,256,256]{2,0,1:T(4,128)(2,1)})) %all-reduce.10.cloned.1.call-update) | async-done | bytes 1048592 | tf_op jit(solution)/shard_map/psum | solution.py:99
  314.2 1.7 convolution_convert_fusion
  316.9 1.3 gather_fusion.3
  318.2 2.0 gather_fusion.5
  321.0 1.3 fusion.23
  322.5 40.7 %gather_fusion.18 = bf16[4096,256]{1,0:T(8,128)(2,1)} fusion(bf16[16,256,256]{2,1,0:T(8,128)(2,1)S(1)} %gather_fusion.7, s32[4096]{0:T(1024)S(1)} %bitcast.154), kind=kCustom, calls=%fused_computation.18 | custom fusion | bytes 4227072 | tf_op jit(solution)/shard_map/vmap()/gather | solution.py:51
  363.2 2.0 gather_fusion.4
  365.2 16.1 %copy_select_fusion = (bf16[16,256,256]{2,0,1:T(8,128)(2,1)}, bf16[16,256,256]{2,0,1:T(8,128)(2,1)S(1)}) fusion(bf16[16,256,256]{2,1,0:T(8,128)(2,1)} %gather_fusion.4, pred[16]{0:T(512)(128)(4,1)S(1)} %iota_compare_fusion.3, pred[16]{0:T(512)(128)(4,1)S(1)} %copy-done.13, bf16[1,1,16,256,256]{4,3,2,1,0:T(8,128)(2,1)S(1)} %copy-done.1, ...), kind=kLoop, calls=%fused_computation.46 | loop fusion | flops 4194304 | bytes 12587056 | tf_op jit(solution)/shard_map/jit(_where)/select_n | solution.py:154
  381.2 0.8 copy.59
  382.6 0.7 copy-done.3
  383.3 2.3 copy.61
  386.2 1.2 broadcast_select_fusion.2
  387.5 1.3 sort.65
  389.5 61.3 %all-reduce.6.cloned.1.call-done = bf16[3,256,256]{2,1,0:T(8,128)(2,1)} async-done(((bf16[3,256,256]{2,1,0:T(8,128)(2,1)}), bf16[3,256,256]{2,1,0:T(8,128)(2,1)}) %all-reduce.6.cloned.1.call-update) | async-done | bytes 393232 | tf_op jit(solution)/shard_map/psum | solution.py:36
  451.5 3.0 gather_fusion.13
  454.5 3.3 collective-permute-start.1
  457.8 119.4 %all-reduce.8.cloned.1.call-done = bf16[3,256,256]{2,1,0:T(8,128)(2,1)} async-done(((bf16[3,256,256]{2,1,0:T(8,128)(2,1)}), bf16[3,256,256]{2,1,0:T(8,128)(2,1)}) %all-reduce.8.cloned.1.call-update) | async-done | bytes 393232 | tf_op jit(solution)/shard_map/psum | solution.py:36
  577.2 2.4 gather_fusion.15
  579.6 3.3 collective-permute-start.2
  585.8 5.3 collective-permute-start
  591.7 3.3 collective-permute-start.3
  595.7 1.6 scatter_fusion
  597.3 1.4 collective-permute-done.3
  598.7 0.8 copy-done.5
  599.6 23.9 %while.23 = (s32[]{:T(128)}, bf16[4,256,256]{2,1,0:T(8,128)(2,1)S(1)}, s32[]{:T(128)}, bf16[4,256,256]{2,1,0:T(8,128)(2,1)}, bf16[4,256,256]{2,1,0:T(8,128)(2,1)...) while((s32[]{:T(128)}, ...), condition=%wide.region_27.28_spmd, body=%wide.region_25.27_spmd.sunk | while | flops 33816600 | bytes 657126 | solution.py:180
  602.8 0.8 and_reduce_fusion.5
  603.6 1.8 fusion.73
  608.6 0.8 and_reduce_fusion.5
  609.4 1.8 fusion.73
  614.4 0.8 and_reduce_fusion.5
  615.2 1.8 fusion.73
  620.2 0.8 and_reduce_fusion.5
  621.0 1.8 fusion.73
  623.4 3.3 collective-permute-start.4
  626.8 50.8 %while.22 = (s32[]{:T(128)}, bf16[16,256,256]{2,1,0:T(8,128)(2,1)S(1)}, s32[]{:T(128)}, s32[16]{0:T(128)S(1)}, bf16[16,256,256]{2,1,0:T(8,128)(2,1)}, /*index=5*...) while((s32[]{:T(128)}, ...), condition=%wide.region_24.25_spmd, body=%wide.region_22.24_spmd.sunk | while | flops 33816608 | bytes 656746 | solution.py:188
  634.4 0.8 and_reduce_fusion.4
  635.2 1.8 fusion.70
  644.6 0.8 and_reduce_fusion.4
  645.3 1.8 fusion.70
  654.7 0.8 and_reduce_fusion.4
  655.5 1.8 fusion.70
  664.9 0.8 and_reduce_fusion.4
  665.7 1.8 fusion.70
  675.1 0.8 and_reduce_fusion.4
  675.8 1.8 fusion.70
  677.6 1.4 gather_fusion.17
  679.0 1.3 broadcast_select_fusion
  680.3 0.7 scatter_fusion.1
  681.0 1.3 copy-done.2
  (144 shorter events, 24.6 us)
Async XLA Ops:
  7.9 313.1 %all-to-all-start = ((bf16[32,256,8]{1,2,0:T(8,128)(2,1)}), bf16[32,256,8]{1,2,0:T(8,128)(2,1)S(1)}, u32[]{:S(2)}, u32[]{:S(2)}) async-start(bf16[32,256,8]{1,2,0:T(8,128)(2,1)} %broadcast_in_dim.201), calls=%async_computation | async-start | bytes 262144 | tf_op jit(solution)/shard_map/all_to_all | solution.py:24
  23.2 290.9 %all-reduce.10.cloned.1.call-start = ((), (), s32[]{:S(2)}) async-start(), calls=%async_computation.3 | async-start | bytes 2097152 | tf_op jit(solution)/shard_map/psum | solution.py:99
  31.9 3.9 copy-start
  35.8 2.1 copy-start.4
  40.1 69.3 %copy-start.16 = (s32[1,1,16]{2,1,0:T(1,128)S(1)}, s32[1,1,16]{2,1,0:T(1,128)}, u32[]{:S(2)}) copy-start(s32[1,1,16]{2,1,0:T(1,128)} %param.15) | copy-start | bytes 196
  40.1 410.7 %all-reduce.6.cloned.1.call-start = ((), (), s32[]{:S(2)}) async-start(), calls=%async_computation.1 | async-start | bytes 786432 | tf_op jit(solution)/shard_map/psum | solution.py:36
  106.7 1.3 copy-start.19
  108.1 28.3 %copy-start.10 = (s32[3]{0:T(128)}, s32[3]{0:T(128)S(1)}, u32[]{:S(2)}) copy-start(s32[3]{0:T(128)S(1)} %compare_select_fusion.5) | copy-start | bytes 40
  109.4 27.0 %copy-start.14 = (pred[3]{0:T(512)(128)(4,1)}, pred[3]{0:T(512)(128)(4,1)S(1)}, u32[]{:S(2)}) copy-start(pred[3]{0:T(512)(128)(4,1)S(1)} %gather_fusion.8) | copy-start | bytes 13
  135.6 0.8 copy-start.21
  137.9 23.4 %copy-start.9 = (bf16[16,256]{1,0:T(8,128)(2,1)S(1)}, bf16[16,256]{1,0:T(8,128)(2,1)}, u32[]{:S(2)}) copy-start(bf16[16,256]{1,0:T(8,128)(2,1)} %param.19) | copy-start | bytes 24580
  314.2 1.9 copy-start.6
  320.3 0.7 copy-start.20
  363.2 2.0 copy-start.1
  363.2 2.0 copy-start.12
  363.2 2.0 copy-start.13
  382.0 1.3 copy-start.3
  383.3 2.9 copy-start.15
  385.6 1.9 copy-start.18
  385.6 3.8 copy-start.22
  387.4 195.5 %copy-start.17 = (pred[16]{0:T(512)(128)(4,1)S(1)}, pred[16]{0:T(512)(128)(4,1)}, u32[]{:S(2)}) copy-start(pred[16]{0:T(512)(128)(4,1)} %get-tuple-element.226) | copy-start | bytes 52
  387.4 208.3 %copy-start.11 = (s32[3]{0:T(128)S(1)}, s32[3]{0:T(128)}, u32[]{:S(2)}) copy-start(s32[3]{0:T(128)} %copy-done.10) | copy-start | bytes 40
  387.4 189.8 %all-reduce.8.cloned.1.call-start = ((), (), s32[]{:S(2)}) async-start(), calls=%async_computation.2 | async-start | bytes 786432 | tf_op jit(solution)/shard_map/psum | solution.py:36
  451.5 148.0 %copy-start.8 = (s32[3]{0:T(128)S(1)}, s32[3]{0:T(128)}, u32[]{:S(2)}) copy-start(s32[3]{0:T(128)} %constant.175.clone.1) | copy-start | bytes 40
  454.5 144.2 %collective-permute-start.1 = (bf16[4,256,256]{2,1,0:T(8,128)(2,1)}, bf16[4,256,256]{2,1,0:T(8,128)(2,1)S(1)}, u32[]{:S(2)}, u32[]{:S(2)}) collective-permute-start(bf16[4,256,256]{2,1,0:T(8,128)(2,1)} %gather_fusion.13), channel_id=1, source_target_pairs={{0,256},{256,0},{32,288},{288,32},{64,320},{320,64},{96,352},{352,... | collective-permute-start | bytes 1572872 | tf_op jit(solution)/shard_map/ppermute | solution.py:47
  579.6 19.9 %collective-permute-start.2 = (bf16[4,256,256]{2,1,0:T(8,128)(2,1)}, bf16[4,256,256]{2,1,0:T(8,128)(2,1)}, u32[]{:S(2)}, u32[]{:S(2)}) collective-permute-start(bf16[4,256,256]{2,1,0:T(8,128)(2,1)} %gather_fusion.15), channel_id=1, source_target_pairs={{0,256},{256,0},{32,288},{288,32},{64,320},{320,64},{96,352},{352,... | collective-permute-start | bytes 1572872 | tf_op jit(solution)/shard_map/ppermute | solution.py:47
  585.8 11.5 %collective-permute-start = (s32[]{:T(128)}, s32[]{:T(128)}, u32[]{:S(2)}, u32[]{:S(2)}) collective-permute-start(s32[]{:T(128)} %select_n.307), channel_id=1, source_target_pairs={{0,256},{256,0},{32,288},{288,32},{64,320},{320,64},{96,352},{352,... | collective-permute-start | bytes 20 | tf_op jit(solution)/shard_map/ppermute | solution.py:47
  591.7 7.0 %collective-permute-start.3 = (s32[4]{0:T(128)S(1)}, s32[4]{0:T(128)S(1)}, u32[]{:S(2)}, u32[]{:S(2)}) collective-permute-start(s32[4]{0:T(128)S(1)} %gather_fusion.16), channel_id=1, source_target_pairs={{0,256},{256,0},{32,288},{288,32},{64,320},{320,64},{96,352},{352,... | collective-permute-start | bytes 56 | tf_op jit(solution)/shard_map/ppermute | solution.py:47
  597.3 29.5 %copy-start.7 = (s32[3]{0:T(128)S(1)}, s32[3]{0:T(128)}, u32[]{:S(2)}) copy-start(s32[3]{0:T(128)} %constant.168.clone.1) | copy-start | bytes 40
  598.7 0.8 copy-start.5
  623.4 55.6 %collective-permute-start.4 = (bf16[4,256,256]{2,1,0:T(8,128)(2,1)S(1)}, bf16[4,256,256]{2,1,0:T(8,128)(2,1)}, u32[]{:S(2)}, u32[]{:S(2)}) collective-permute-start(bf16[4,256,256]{2,1,0:T(8,128)(2,1)S(1)} %get-tuple-element.124), channel_id=1, source_target_pairs={{0,256},{256,0},{32,288},{288,32},{64,320},{320,64},{96,352},{352,... | collective-permute-start | bytes 1572872 | tf_op jit(solution)/shard_map/ppermute | solution.py:47
  681.0 1.3 copy-start.2
Sparse Core Ops, SparseCore 0:
  40.2 273.9 all-reduce.9
  387.5 63.2 all-reduce.5
  453.8 123.4 all-reduce.7
where the time goes:
time: 691 us; the launch traced here: 689 us
  waiting for transfers between devices  298 us (43%)
  blocking collectives  128 us (19%)
  local copies, waits for them, and re-layouts  114 us (16%)
  loops' own time  39.3 us (6%)
  starting transfers between devices  34.1 us (5%)
  other arithmetic  33.2 us (5%)
  matrix products  25.1 us (4%)
  between operations  17.1 us (2%)
    psum x2, waiting for transfers between devices, spread(): shard = lax.psum(shard, axis)  181 us
    psum x1, waiting for transfers between devices, body(): lax.psum(new_part.astype(jnp.bfloat16), 'prow').astype(jnp.float32)  116 us
    psum x1, blocking collectives, body(): lax.psum(id_part.astype(jnp.bfloat16), 'prow').astype(jnp.float32)  64.7 us
    gather x2, local copies, waits for them, and re-layouts, pick_rows(): return tile[rows]  40.7 us
    all_gather x1, blocking collectives, body(): upper_inv = lax.all_gather(u_inverse, 'prow', axis=0, tiled=True)  36.9 us
    another operation x1, loops' own time, body(): result = lax.fori_loop(0, (needed + 1) // 2, even_step, result)  28.3 us
    psum x2, blocking collectives, spread(): shard = lax.psum(shard, axis)  26.1 us
    gather x1, local copies, waits for them, and re-layouts, body(): anchor = anchor_top[row_index]  23 us
  transfers between devices with their start and end apart: 9, of which 4 were waited for; matrix products, arithmetic and copies ran while one was open for 13% of the time, Pallas kernels for 0%

commit v1 on v0

v1 whole, which is shorter than its diff:
```python
import jax
import jax.numpy as jnp
from jax import lax
from jax.experimental import pallas as pl
from jax.experimental.pallas import tpu as pltpu
from jax.sharding import PartitionSpec as P

MESH = pl.DeviceIdType.MESH
SIDE = 256
SLOTS = 16
ROW0 = 13
COL0 = 5
BF = jnp.bfloat16
F32 = jnp.float32
VM = pltpu.VMEM


def div(a, b):
    return lax.div(a, jnp.int32(b))


def rem(a, b):
    return lax.rem(a, jnp.int32(b))


def prepare_kernel(ids, counts, piv, tiles, newp, oldp, lowp, corner, table):
    p = lax.axis_index("prow")
    q = lax.axis_index("pcol")
    rows = [0, ROW0, ROW0 + 1, ROW0 + 2]
    cols = [COL0, COL0 + 1, COL0 + 2, 0]
    for r in rows:
        for c in cols:
            table[r * 8 + c] = -1
    for s in range(SLOTS):

        @pl.when(s < counts[0, 0])
        def _():
            table[ids[0, 0, s]] = s

    def tile_at(r, c):
        slot = table[r * 8 + c]
        tile = tiles[0, 0, jnp.maximum(slot, 0)]
        return jnp.where(slot >= 0, tile, jnp.zeros_like(tile))

    lane = lax.broadcasted_iota(jnp.int32, (SIDE, SIDE), 1)
    wanted = piv[...]
    hots = [(wanted == (p + 16 * r) * SIDE + lane).astype(BF) for r in rows]

    def new_column(m, c):
        acc = jnp.zeros((SIDE, SIDE), F32)
        for hot, r in zip(hots, rows):
            acc += jnp.dot(hot, tile_at(r, c), preferred_element_type=F32)
        newp[m] = acc.astype(BF)

    def step(m, carry):
        new_column(m, COL0 + m)
        return carry

    lax.fori_loop(0, 3, step, 0)

    @pl.when(q == 0)
    def _():
        new_column(3, 0)
        for k in range(3):
            lowp[k] = tile_at(ROW0 + k, 0)

    @pl.when(p == 0)
    def _():
        for m in range(3):
            oldp[m] = tile_at(0, COL0 + m)

    @pl.when((p == 0) & (q == 0))
    def _():
        corner[...] = tile_at(0, 0)


TREE = [(4, 0), (2, 0), (1, 0), (6, 4), (5, 4), (3, 2), (7, 6)]


def exchange_kernel(
    newp, oldp, lowp, corner, l_part, u_part,
    both, low, obuf, lbuf, ubuf,
    r1, a1, r2, a2, r3, ro1, ssem, rsem, lsem,
):
    p = lax.axis_index("prow")
    q = lax.axis_index("pcol")
    y, h, c = div(p, 4), rem(div(p, 2), 2), rem(p, 2)
    x, z = div(q, 8), rem(q, 8)
    isq0 = q == 0
    isp0 = p == 0
    corner_dev = isq0 & isp0

    def P_(yy, hh, cc):
        return yy * 4 + hh * 2 + cc

    ys = [rem(y + d, 4) for d in (1, 2, 3)]
    xs = [rem(x + d, 4) for d in (1, 2, 3)]
    zs = [rem(z + d, 8) for d in range(1, 8)]
    d_y = [(P_(v, h, c), q) for v in ys]
    d_h = (P_(y, 1 - h, c), q)
    d_c = (P_(y, h, 1 - c), q)
    d_x = [(p, v * 8 + z) for v in xs]
    d_z = [(p, x * 8 + v) for v in zs]

    bar = pltpu.get_barrier_semaphore()
    greet = d_y + [d_h, d_c] + d_x + d_z
    for dev in greet:
        pl.semaphore_signal(bar, inc=1, device_id=dev, device_id_type=MESH)
    pl.semaphore_wait(bar, len(greet))

    pend = []
    counter = [0, 0]

    def when(cond, fn):
        if cond is None:
            fn()
        else:
            pl.when(cond)(fn)

    def sems(n):
        base = counter[1]
        counter[1] += n
        return [rsem.at[base + i] for i in range(n)]

    def send(src, dst, rs, dev, cond=None):
        d = pltpu.make_async_remote_copy(
            src_ref=src, dst_ref=dst, send_sem=ssem.at[counter[0]], recv_sem=rs,
            device_id=dev, device_id_type=MESH)
        counter[0] += 1
        when(cond, d.start)
        pend.append((cond, d))

    def recv(dst, rs, cond=None):
        d = pltpu.make_async_remote_copy(
            src_ref=dst, dst_ref=dst, send_sem=ssem.at[0], recv_sem=rs,
            device_id=d_c, device_id_type=MESH)
        when(cond, d.wait_recv)

    def al(v, n):
        return pl.multiple_of(v, n)

    def rows32(cc, yy):
        return pl.ds(al(cc * 128 + yy * 32, 32), 32)

    def quarter(v):
        return pl.ds(al(v * 64, 64), 64)

    groups = [(0, 3, None), (3, 1, isq0)]
    gather_groups = [(0, 6, None), (6, 1, isq0)]

    s_n1, s_n2, s_n3 = sems(2), sems(6), sems(2)
    s_n4, s_n5 = sems(6), sems(8)
    s_o1, s_o2, s_o3 = sems(1), sems(1), sems(1)
    s_b1, s_b2, s_b3 = sems(3), sems(3), sems(9)
    s_z1, s_zh, s_z2, s_z3, s_z4, s_z5 = sems(1), sems(1), sems(1), sems(1), sems(3), sems(1)
    s_l1, s_l2 = sems(7), sems(3)
    s_u1, s_u2, s_u3 = sems(1), sems(3), sems(1)

    own_l = pltpu.make_async_copy(l_part, lbuf.at[q], lsem.at[0])
    own_u = pltpu.make_async_copy(u_part, ubuf.at[y, h, c], lsem.at[1])
    own_low = pltpu.make_async_copy(lowp, low, lsem.at[2])
    own_o = pltpu.make_async_copy(corner, obuf, lsem.at[3])
    own_old = pltpu.make_async_copy(oldp.at[:, pl.ds(0, 128)], ro1, lsem.at[4])
    own_l.start()
    own_u.start()
    when(corner_dev, own_o.start)
    when(isq0, own_low.start)
    when(isp0, own_old.start)

    for i, (g, n, cond) in enumerate(groups):
        send(newp.at[pl.ds(g, n), pl.ds(al((1 - c) * 128, 128), 128)], r1.at[pl.ds(g, n)], s_n1[i], d_c, cond)
    send(oldp.at[:, pl.ds(128, 128)], ro1, s_o1[0], d_c, isp0)
    when(corner_dev, own_o.wait)
    rootz = (x == 0) & (z == 0) & (h == 0) & (c == 0)
    for i in range(3):
        send(obuf.at[quarter(ys[i])], obuf.at[quarter(ys[i])], s_z1[0], d_y[i], corner_dev)
    send(obuf.at[quarter(y)], obuf.at[quarter(y)], s_zh[0], d_h, corner_dev)
    own_u.wait()
    send(ubuf.at[y, h, c], ubuf.at[y, h, c], s_u1[0], d_h)
    own_l.wait()
    for i in range(7):
        send(lbuf.at[q], lbuf.at[q], s_l1[i], d_z[i])
    when(isq0, own_low.wait)
    for j in range(3):
        for i in range(3):
            send(low.at[j, quarter(xs[i])], low.at[j, quarter(xs[i])], s_b1[j], d_x[i], isq0)

    def low_tree(parent):
        for j in range(3):
            for child, par in TREE:
                if par == parent:
                    send(low.at[j, quarter(x)], low.at[j, quarter(x)], s_b2[j], (p, x * 8 + child),
                         (z == parent) & (x == 0) if parent == 0 else (z == parent))

    low_tree(0)

    for i, (g, n, cond) in enumerate(groups):
        recv(r1.at[pl.ds(g, n)], s_n1[i], cond)
    a1[...] = newp[:, pl.ds(al(c * 128, 128), 128)] + r1[...]
    for d in range(3):
        for i, (g, n, cond) in enumerate(groups):
            send(a1.at[pl.ds(g, n), pl.ds(al(ys[d] * 32, 32), 32)], r2.at[d, pl.ds(g, n)], s_n2[2 * d + i], d_y[d], cond)
    recv(ro1, s_o1[0], p == 1)
    when(isp0, own_old.wait)
    oldroot = (y == 0) & (h == 0)
    for d in range(3):
        send(ro1.at[:, pl.ds(al(ys[d] * 32, 32), 32)], both.at[pl.ds(3, 3), rows32(c, ys[d])], s_o2[0], d_y[d], oldroot)

    @pl.when(oldroot)
    def _():
        both[pl.ds(3, 3), rows32(c, 0)] = ro1[:, pl.ds(0, 32)]

    second = (x > 0) & (z == 0)
    for j in range(3):
        recv(low.at[j, quarter(x)], s_b1[j], second)
        for child, par in TREE:
            if par == 0:
                send(low.at[j, quarter(x)], low.at[j, quarter(x)], s_b2[j], (p, x * 8 + child), second)
    recv(obuf.at[quarter(y)], s_z1[0], rootz & (y > 0))
    send(obuf.at[quarter(y)], obuf.at[quarter(y)], s_zh[0], d_h, rootz & (y > 0))

    for d in range(3):
        for i, (g, n, cond) in enumerate(groups):
            recv(r2.at[d, pl.ds(g, n)], s_n2[2 * d + i], cond)
    a2[...] = a1[:, pl.ds(al(y * 32, 32), 32)] + r2[0] + r2[1] + r2[2]
    for i, (g, n, cond) in enumerate(groups):
        send(a2.at[pl.ds(g, n)], r3.at[pl.ds(g, n)], s_n3[i], d_h, cond)
    recv(both.at[pl.ds(3, 3), rows32(c, y)], s_o2[0], (h == 0) & (y > 0))
    send(both.at[pl.ds(3, 3), rows32(c, y)], both.at[pl.ds(3, 3), rows32(c, y)], s_o3[0], d_h, h == 0)

    ox = (x == 0) & (c == 0)
    recv(obuf.at[quarter(y)], s_zh[0], ox & (z == 0) & (h == 1))

    def corner_tree(parent):
        for child, par in TREE:
            if par == parent:
                send(obuf.at[quarter(y)], obuf.at[quarter(y)], s_z2[0], (p, x * 8 + child), ox & (z == parent))

    corner_tree(0)
    for j in range(3):
        recv(low.at[j, quarter(x)], s_b2[j], z > 0)
    for parent in (4, 2, 6):
        low_tree(parent)

    root_low = (x == 0) & (z == 0)
    for j in range(3):
        for i in range(3):
            send(low.at[j, quarter(x)], low.at[j, quarter(x)], s_b3[3 * j + i], d_x[i],
                 jnp.logical_not((xs[i] == 0) & (z == 0)))

    for i in range(7):
        recv(lbuf.at[q], s_l1[i])
    for i in range(3):
        send(lbuf.at[pl.ds(x * 8, 8)], lbuf.at[pl.ds(x * 8, 8)], s_l2[i], d_x[i])
    recv(ubuf.at[y, h, c], s_u1[0])
    for i in range(3):
        send(ubuf.at[y, :, c], ubuf.at[y, :, c], s_u2[i], d_y[i])

    recv(obuf.at[quarter(y)], s_z2[0], ox & (z > 0))
    for parent in (4, 2, 6):
        corner_tree(parent)
    for i in range(3):
        send(obuf.at[quarter(y)], obuf.at[quarter(y)], s_z3[0], d_x[i], ox)

    for i, (g, n, cond) in enumerate(groups):
        recv(r3.at[pl.ds(g, n)], s_n3[i], cond)
    both[pl.ds(0, 3), rows32(c, y)] = a2[pl.ds(0, 3)] + r3[pl.ds(0, 3)]

    @pl.when(isq0)
    def _():
        both[6, rows32(c, y)] = a2[3] + r3[3]

    recv(both.at[pl.ds(3, 3), rows32(c, y)], s_o3[0], h == 1)
    for d in range(3):
        for i, (g, n, cond) in enumerate(gather_groups):
            send(both.at[pl.ds(g, n), rows32(c, y)], both.at[pl.ds(g, n), rows32(c, y)], s_n4[2 * d + i], d_y[d], cond)
    for i, (g, n, cond) in enumerate(gather_groups):
        send(both.at[pl.ds(g, n), rows32(c, y)], both.at[pl.ds(g, n), rows32(c, y)], s_n5[i], d_c, cond)
    recv(obuf.at[quarter(y)], s_z3[0], (x > 0) & (c == 0))
    for i in range(3):
        send(obuf.at[quarter(y)], obuf.at[quarter(y)], s_z4[i], d_y[i],
             (c == 0) & jnp.logical_not(isq0 & (ys[i] == 0) & (h == 0)))
    for d in range(3):
        src = rem(y + 3 - d, 4)
        for i, (g, n, cond) in enumerate(gather_groups):
            recv(both.at[pl.ds(g, n), rows32(c, src)], s_n4[2 * d + i], cond)
            send(both.at[pl.ds(g, n), rows32(c, src)], both.at[pl.ds(g, n), rows32(c, src)],
                 s_n5[2 * (d + 1) + i], d_c, cond)
    for i in range(3):
        recv(obuf.at[quarter(rem(y + 3 - i, 4))], s_z4[i], (c == 0) & jnp.logical_not(corner_dev))
    send(obuf, obuf, s_z5[0], d_c, c == 0)
    for i in range(3):
        recv(ubuf.at[rem(y + 3 - i, 4), :, c], s_u2[i])
    send(ubuf.at[:, :, c], ubuf.at[:, :, c], s_u3[0], d_c)

    for j in range(3):
        for i in range(3):
            recv(low.at[j, quarter(rem(x + 3 - i, 4))], s_b3[3 * j + i], jnp.logical_not(root_low))
    for i in range(3):
        recv(lbuf.at[pl.ds(rem(x + 3 - i, 4) * 8, 8)], s_l2[i])
    recv(obuf, s_z5[0], c == 1)
    recv(ubuf.at[:, :, 1 - c], s_u3[0])
    for d in range(4):
        src = rem(y + 4 - d, 4)
        for i, (g, n, cond) in enumerate(gather_groups):
            recv(both.at[pl.ds(g, n), rows32(1 - c, src)], s_n5[2 * d + i], cond)
    for cond, d in pend:
        when(cond, d.wait_send)


def finish_kernel(ids, counts, piv, both, low, corner, l_t, u_inv, tiles, out, lower, upper):
    p = lax.axis_index("prow")
    q = lax.axis_index("pcol")
    block = pl.program_id(0)
    sub = lax.broadcasted_iota(jnp.int32, (SIDE, SIDE), 0)

    def hot_of(row):
        return piv[...] == (p + 16 * row) * SIDE + sub

    def swap(tile, row, old):
        hot = hot_of(row)
        moved = jnp.max(hot.astype(F32), axis=1, keepdims=True) > 0.5
        moved_rows = jnp.dot(hot.astype(BF), old, preferred_element_type=F32)
        return jnp.where(moved, moved_rows, tile.astype(F32))

    @pl.when(block == 0)
    def _():
        lt = l_t[...].astype(F32).reshape(SIDE, SIDE).astype(BF)
        u = u_inv[...].reshape(SIDE, SIDE)

        def step(k, carry):
            s = swap(low[k], ROW0 + k, corner[...]).astype(BF)
            lower[k] = jnp.dot(s, u, preferred_element_type=F32).astype(BF)
            upper[k] = lax.dot_general(
                lt, both[k], (((0,), (0,)), ((), ())), preferred_element_type=F32
            ).astype(BF)
            return carry

        lax.fori_loop(0, 3, step, 0)

    def slot_step(i, carry):
        s = block * 4 + i
        code = ids[0, 0, s]
        row, col = div(code, 8), rem(code, 8)
        live = s < counts[0, 0]
        low_row = row >= ROW0
        up_col = col >= COL0
        k = jnp.maximum(row - ROW0, 0)
        m = jnp.maximum(col - COL0, 0)
        trail = live & low_row & up_col
        top = live & (p == 0) & (row == 0) & up_col
        first = live & (q == 0) & (col == 0) & low_row
        diag = live & (p == 0) & (q == 0) & (code == 0)
        plain = live & jnp.logical_not(trail | top | first | diag)

        @pl.when(trail)
        def _():
            product = jnp.dot(lower[k], upper[m], preferred_element_type=F32)
            out[0, 0, i] = (swap(tiles[0, 0, i], row, both[3 + m]) - product).astype(BF)

        @pl.when(top)
        def _():
            out[0, 0, i] = upper[m]

        @pl.when(first)
        def _():
            out[0, 0, i] = lower[k]

        @pl.when(diag)
        def _():
            out[0, 0, i] = both[6]

        @pl.when(plain)
        def _():
            out[0, 0, i] = tiles[0, 0, i]

        @pl.when(jnp.logical_not(live))
        def _():
            out[0, 0, i] = jnp.zeros((SIDE, SIDE), BF)

        return carry

    lax.fori_loop(0, 4, slot_step, 0)


def body(tiles, tile_ids, counts, pivots, l_inverse, u_inverse):
    tile = (SIDE, SIDE)
    sds = jax.ShapeDtypeStruct
    vmem = pl.BlockSpec(memory_space=VM)
    smem = pl.BlockSpec(memory_space=pltpu.SMEM)
    newp, oldp, lowp, corner = pl.pallas_call(
        prepare_kernel,
        out_shape=(sds((4, *tile), BF), sds((3, *tile), BF), sds((3, *tile), BF), sds(tile, BF)),
        in_specs=[smem, smem, vmem, vmem],
        out_specs=(vmem,) * 4,
        scratch_shapes=[pltpu.SMEM((128,), jnp.int32)],
        name="prepare",
    )(tile_ids, counts, pivots.reshape(SIDE, 1), tiles)
    l_part = l_inverse.T
    dma = pltpu.SemaphoreType.DMA
    both, low, obuf, lbuf, ubuf = pl.pallas_call(
        exchange_kernel,
        out_shape=(
            sds((7, *tile), BF), sds((3, *tile), BF), sds(tile, BF),
            sds((32, 8, SIDE), BF), sds((4, 2, 2, 16, SIDE), BF),
        ),
        in_specs=[vmem] * 6,
        out_specs=(vmem,) * 5,
        scratch_shapes=[
            VM((4, 128, SIDE), BF), VM((4, 128, SIDE), BF), VM((3, 4, 32, SIDE), BF),
            VM((4, 32, SIDE), BF), VM((4, 32, SIDE), BF), VM((3, 128, SIDE), BF),
            dma((160,)), dma((80,)), dma((5,)),
        ],
        compiler_params=pltpu.CompilerParams(collective_id=0, has_side_effects=True),
        name="exchange",
    )(newp, oldp, lowp, corner, l_part, u_inverse)
    whole = lambda *shape: pl.BlockSpec(shape, lambda i: (0,) * len(shape), memory_space=VM)
    return pl.pallas_call(
        finish_kernel,
        grid=(4,),
        out_shape=sds((1, 1, SLOTS, *tile), BF),
        in_specs=[
            smem, smem, whole(1, SIDE), whole(7, *tile), whole(3, *tile), whole(*tile),
            whole(32, 8, SIDE), whole(16, 16, SIDE),
            pl.BlockSpec((1, 1, 4, *tile), lambda i: (0, 0, i, 0, 0), memory_space=VM),
        ],
        out_specs=pl.BlockSpec((1, 1, 4, *tile), lambda i: (0, 0, i, 0, 0), memory_space=VM),
        scratch_shapes=[VM((3, *tile), BF), VM((3, *tile), BF)],
        name="finish",
    )(tile_ids, counts, pivots.reshape(1, SIDE), both, low, obuf, lbuf, ubuf.reshape(16, 16, SIDE), tiles)


def solution(mesh):
    return jax.shard_map(
        body,
        mesh=mesh,
        in_specs=(
            P("prow", "pcol", None, None, None), P("prow", "pcol", None), P("prow", "pcol"),
            P(), P(None, "pcol"), P("prow", None),
        ),
        out_specs=P("prow", "pcol", None, None, None),
        check_vma=False,
    )
```

time: 691 us -> 63.7 us (0.09)
  the two profiles are of different devices: /device:TPU:24 before, /device:TPU:487 now
where the time goes in v1:
time: 63.7 us; the launch traced here: 63.2 us
  Pallas kernels  61.1 us (96%)
  local copies, waits for them, and re-layouts  1.48 us (2%)
  between operations  0.66 us (1%)
    pallas_call x1, Pallas kernels, body(): pl.pallas_call(exchange_kernel, out_shape=(sds((7, *tile), BF), sds((3, *...  50.6 us
    pallas_call x1, Pallas kernels, body(): pl.pallas_call(finish_kernel, grid=(4,), out_shape=sds((1, 1, SLOTS, *til...  6.63 us
    pallas_call x1, Pallas kernels, body(): pl.pallas_call(prepare_kernel, out_shape=(sds((4, *tile), BF), sds((3, *t...  3.92 us
    reshape x1, local copies, waits for them, and re-layouts, body(): pivots.reshape(SIDE, 1)  1.48 us

profile of v1, /device:TPU:487, one launch (start us, length us, event | category | flops | bytes accessed | tf_op | source)
XLA Modules:
  0.0 63.2 jit_solution(9358903897478984629)
XLA Ops:
  0.7 1.5 %copy.7.piv = s32[256,1]{1,0:T(8,128)} copy(s32[256,1]{0,1:T(1,128)} %bitcast.6) | data formatting | bytes 2048 | tf_op jit(solution)/shard_map/reshape | solution.py:398
  2.1 3.9 %prepare.1 = (bf16[4,256,256]{2,1,0:T(8,128)(2,1)}, bf16[3,256,256]{2,1,0:T(8,128)(2,1)}, bf16[3,256,256]{2,1,0:T(8,128)(2,1)}, bf16[256,256]{1,0:T(8,128)(2,1)}) custom-call(s32[1,1,16]{2,1,0:T(1,128)} %ids.3, s32[1,1]{1,0:T(1,128)S(6)} %copy.8.counts, s32[256,1]{1,0:T(8,128)} %copy.7.piv, bf16[1,1,16,256,256]{4,3,2,1,0:T(8,128)(2,1)} %tiles.3), custom_call_target="tpu_custom_call" | custom-call | tf_op jit(solution)/shard_map/prepare/pallas_call | solution.py:391
  6.0 50.6 %exchange.1 = (bf16[7,256,256]{2,1,0:T(8,128)(2,1)}, bf16[3,256,256]{2,1,0:T(8,128)(2,1)}, bf16[256,256]{1,0:T(8,128)(2,1)}, bf16[32,8,256]{2,1,0:T(8,128)(2,1)}, bf16[4,2,2,16,256]{4,3,2,1,0:T(8,128)(2,1)}) custom-call(bf16[4,256,256]{2,1,0:T(8,128)(2,1)} %get-tuple-element.14.newp, bf16[3,256,256]{2,1,0:T(8,128)(2,1)} %get-tuple-element.15.oldp, ...), custom_call_target="tpu_custom_call" | custom-call | tf_op jit(solution)/shard_map/exchange/pallas_call | solution.py:401
  56.6 6.6 %finish.1 = bf16[1,1,16,256,256]{4,3,2,1,0:T(8,128)(2,1)} custom-call(s32[1,1,16]{2,1,0:T(1,128)} %ids.3, s32[1,1]{1,0:T(1,128)S(6)} %copy.8.counts, s32[1,256]{1,0:T(1,128)} %bitcast.7, bf16[7,256,256]{2,1,0:T(8,128)(2,1)} %get-tuple-element.18.both, bf16[3,256,256]{2,1,0:T(8,128)(2,1)} %get-tuple-element.19.low, ...), custom_call_target="tpu_custom_call" | custom-call | tf_op jit(solution)/shard_map/finish/pallas_call | solution.py:418

commit v2 on v1

v2 whole, which is shorter than its diff:
```python
import jax
import jax.numpy as jnp
from jax import lax
from jax.experimental import pallas as pl
from jax.experimental.pallas import tpu as pltpu
from jax.sharding import PartitionSpec as P

MESH = pl.DeviceIdType.MESH
SIDE = 256
SLOTS = 16
ROW0 = 13
COL0 = 5
BF = jnp.bfloat16
F32 = jnp.float32
VM = pltpu.VMEM


def div(a, b):
    return lax.div(a, jnp.int32(b))


def rem(a, b):
    return lax.rem(a, jnp.int32(b))


TREE = [(4, 0), (2, 0), (1, 0), (6, 4), (5, 4), (3, 2), (7, 6)]
ROWS = (0, ROW0, ROW0 + 1, ROW0 + 2)
COLS = (COL0, COL0 + 1, COL0 + 2, 0)


def exchange_kernel(
    ids, counts, piv, tiles_hbm, l_part, u_part,
    both, low, obuf, lbuf, ubuf,
    tiles, newp, oldp, r1, a1, r2, a2, r3, ro1, ssem, rsem, lsem,
):
    p = lax.axis_index("prow")
    q = lax.axis_index("pcol")
    y, h, c = div(p, 4), rem(div(p, 2), 2), rem(p, 2)
    x, z = div(q, 8), rem(q, 8)
    isq0 = q == 0
    isp0 = p == 0
    corner_dev = isq0 & isp0

    get_tiles = pltpu.make_async_copy(tiles_hbm.at[0, 0], tiles, lsem.at[0])
    get_l = pltpu.make_async_copy(l_part, lbuf.at[q], lsem.at[1])
    get_u = pltpu.make_async_copy(u_part, ubuf.at[y, h, c], lsem.at[2])
    get_tiles.start()
    get_l.start()
    get_u.start()

    def P_(yy, hh, cc):
        return yy * 4 + hh * 2 + cc

    ys = [rem(y + d, 4) for d in (1, 2, 3)]
    xs = [rem(x + d, 4) for d in (1, 2, 3)]
    d_y = [(P_(v, h, c), q) for v in ys]
    d_h = (P_(y, 1 - h, c), q)
    d_c = (P_(y, h, 1 - c), q)
    d_x = [(p, v * 8 + z) for v in xs]
    d_z = [(p, x * 8 + rem(z + d, 8)) for d in range(1, 8)]
    plane = [(rem(y + k // 4, 4), rem(x + k % 4, 4)) for k in range(1, 16)]
    d_plane = [(P_(v, h, c), w * 8 + z) for v, w in plane]
    d_ring = [(P_(y, rem(h + k // 8, 2), c), x * 8 + rem(z + k % 8, 8)) for k in range(1, 16)]

    bar = pltpu.get_barrier_semaphore()
    greet = d_plane + d_ring + [d_c]
    for dev in greet:
        pl.semaphore_signal(bar, inc=1, device_id=dev, device_id_type=MESH)

    def look(s, found):
        code = jnp.where(s < counts[0, 0], ids[0, 0, s], -1)
        return tuple(
            jnp.where(code == ROWS[i // 4] * 8 + COLS[i % 4], s, f) for i, f in enumerate(found)
        )

    slots = lax.fori_loop(0, SLOTS, look, (jnp.int32(-1),) * 16)

    def tile_at(i, j):
        slot = slots[4 * i + j]
        tile = tiles[jnp.maximum(slot, 0)]
        return jnp.where(slot >= 0, tile, jnp.zeros_like(tile))

    sub = lax.broadcasted_iota(jnp.int32, (SIDE, SIDE), 0)
    lane = lax.broadcasted_iota(jnp.int32, (SIDE, SIDE), 1)
    wanted = jnp.sum(jnp.where(sub == lane, piv[...].astype(F32), 0.0), axis=1, keepdims=True)
    hots = [
        (wanted == ((p + 16 * r) * SIDE + lane).astype(F32)).astype(F32).astype(BF) for r in ROWS
    ]
    get_tiles.wait()

    def new_column(m):
        acc = jnp.dot(hots[0], tile_at(0, m), preferred_element_type=F32)
        for i in range(1, 4):
            acc += jnp.dot(hots[i], tile_at(i, m), preferred_element_type=F32)
        newp[m] = acc.astype(BF)

    for m in range(3):
        new_column(m)

    @pl.when(isq0)
    def _():
        new_column(3)
        for k in range(3):
            low[k] = tile_at(1 + k, 3)

    @pl.when(isp0)
    def _():
        for m in range(3):
            old = tile_at(0, m)
            oldp[m] = old
            ro1[m] = old[:128]

    @pl.when(corner_dev)
    def _():
        obuf[...] = tile_at(0, 3).reshape(16, 16, SIDE)

    pl.semaphore_wait(bar, len(greet))

    pend = []
    counter = [0, 0]

    def when(cond, fn):
        if cond is None:
            fn()
        else:
            pl.when(cond)(fn)

    def sems(n):
        base = counter[1]
        counter[1] += n
        return [rsem.at[base + i] for i in range(n)]

    def send(src, dst, rs, dev, cond=None):
        d = pltpu.make_async_remote_copy(
            src_ref=src, dst_ref=dst, send_sem=ssem.at[counter[0]], recv_sem=rs,
            device_id=dev, device_id_type=MESH)
        counter[0] += 1
        when(cond, d.start)
        pend.append((cond, d))

    def recv(dst, rs, cond=None):
        d = pltpu.make_async_remote_copy(
            src_ref=dst, dst_ref=dst, send_sem=ssem.at[0], recv_sem=rs,
            device_id=d_c, device_id_type=MESH)
        when(cond, d.wait_recv)

    def al(v, n):
        return pl.multiple_of(v, n)

    def rows32(cc, yy):
        return pl.ds(al(cc * 128 + yy * 32, 32), 32)

    def quarter(v):
        return pl.ds(al(v * 64, 64), 64)

    groups = [(0, 3, None), (3, 1, isq0)]
    gather_groups = [(0, 6, None), (6, 1, isq0)]

    s_n1, s_n2, s_n3 = sems(2), sems(6), sems(2)
    s_n4, s_n5 = sems(6), sems(8)
    s_o1, s_o2, s_o3 = sems(1), sems(1), sems(1)
    s_b1, s_b2, s_b3 = sems(3), sems(3), sems(9)
    s_c1, s_c2, s_c3, s_c4 = sems(1), sems(1), sems(15), sems(1)
    s_l1, s_l2 = sems(7), sems(3)
    s_u1, s_u2, s_u3 = sems(1), sems(3), sems(1)

    for i, (g, n, cond) in enumerate(groups):
        send(newp.at[pl.ds(g, n), pl.ds(al((1 - c) * 128, 128), 128)], r1.at[pl.ds(g, n)], s_n1[i], d_c, cond)
    send(oldp.at[:, pl.ds(128, 128)], ro1, s_o1[0], d_c, isp0)
    mine = y * 4 + x
    for i, (v, w) in enumerate(plane):
        send(obuf.at[v * 4 + w], obuf.at[v * 4 + w], s_c1[0], d_plane[i], corner_dev)
    source = (z == 0) & (h == 0) & (c == 0)
    for dev in d_ring:
        send(obuf.at[mine], obuf.at[mine], s_c2[0], dev, corner_dev)
    get_u.wait()
    send(ubuf.at[y, h, c], ubuf.at[y, h, c], s_u1[0], d_h)
    get_l.wait()
    for i in range(7):
        send(lbuf.at[q], lbuf.at[q], s_l1[i], d_z[i])
    for j in range(3):
        for i in range(3):
            send(low.at[j, quarter(xs[i])], low.at[j, quarter(xs[i])], s_b1[j], d_x[i], isq0)

    def low_tree(j, parent, cond):
        for child, par in TREE:
            if par == parent:
                send(low.at[j, quarter(x)], low.at[j, quarter(x)], s_b2[j], (p, x * 8 + child), cond)

    def low_ring(j, cond):
        for i in range(3):
            send(low.at[j, quarter(x)], low.at[j, quarter(x)], s_b3[3 * j + i], d_x[i], cond(xs[i]))

    for j in range(3):
        low_tree(j, 0, isq0)

    for i, (g, n, cond) in enumerate(groups):
        recv(r1.at[pl.ds(g, n)], s_n1[i], cond)
    a1[...] = newp[:, pl.ds(al(c * 128, 128), 128)] + r1[...]
    for d in range(3):
        for i, (g, n, cond) in enumerate(groups):
            send(a1.at[pl.ds(g, n), pl.ds(al(ys[d] * 32, 32), 32)], r2.at[d, pl.ds(g, n)], s_n2[2 * d + i], d_y[d], cond)
    recv(ro1, s_o1[0], p == 1)
    oldroot = (y == 0) & (h == 0)
    for d in range(3):
        send(ro1.at[:, pl.ds(al(ys[d] * 32, 32), 32)], both.at[pl.ds(3, 3), rows32(c, ys[d])], s_o2[0], d_y[d], oldroot)

    @pl.when(oldroot)
    def _():
        both[pl.ds(3, 3), rows32(c, 0)] = ro1[:, pl.ds(0, 32)]

    relay = source & jnp.logical_not(corner_dev)
    recv(obuf.at[mine], s_c1[0], relay)
    for dev in d_ring:
        send(obuf.at[mine], obuf.at[mine], s_c2[0], dev, relay)
    second = (x > 0) & (z == 0)
    for j in range(3):
        recv(low.at[j, quarter(x)], s_b1[j], second)
        low_tree(j, 0, second)
    for j in range(3):
        low_ring(j, lambda w: (z == 0) & (w > 0))

    for d in range(3):
        for i, (g, n, cond) in enumerate(groups):
            recv(r2.at[d, pl.ds(g, n)], s_n2[2 * d + i], cond)
    a2[...] = a1[:, pl.ds(al(y * 32, 32), 32)] + r2[0] + r2[1] + r2[2]
    for i, (g, n, cond) in enumerate(groups):
        send(a2.at[pl.ds(g, n)], r3.at[pl.ds(g, n)], s_n3[i], d_h, cond)
    recv(both.at[pl.ds(3, 3), rows32(c, y)], s_o2[0], (h == 0) & (y > 0))
    send(both.at[pl.ds(3, 3), rows32(c, y)], both.at[pl.ds(3, 3), rows32(c, y)], s_o3[0], d_h, h == 0)

    for i in range(7):
        recv(lbuf.at[q], s_l1[i])
    for i in range(3):
        send(lbuf.at[pl.ds(x * 8, 8)], lbuf.at[pl.ds(x * 8, 8)], s_l2[i], d_x[i])
    recv(ubuf.at[y, h, c], s_u1[0])
    for i in range(3):
        send(ubuf.at[y, :, c], ubuf.at[y, :, c], s_u2[i], d_y[i])
    odd = rem(z, 2) == 1
    even = (z > 0) & (rem(z, 2) == 0)
    for j in range(3):
        recv(low.at[j, quarter(x)], s_b2[j], even)
        for parent in (4, 2, 6):
            low_tree(j, parent, z == parent)
    for j in range(3):
        low_ring(j, lambda w: even)

    recv(obuf.at[mine], s_c2[0], (c == 0) & jnp.logical_not(source))
    for i, (v, w) in enumerate(plane):
        send(obuf.at[mine], obuf.at[mine], s_c3[i], d_plane[i],
             (c == 0) & jnp.logical_not((z == 0) & (h == 0) & (v == 0) & (w == 0)))

    for i, (g, n, cond) in enumerate(groups):
        recv(r3.at[pl.ds(g, n)], s_n3[i], cond)
    both[pl.ds(0, 3), rows32(c, y)] = a2[pl.ds(0, 3)] + r3[pl.ds(0, 3)]

    @pl.when(isq0)
    def _():
        both[6, rows32(c, y)] = a2[3] + r3[3]

    recv(both.at[pl.ds(3, 3), rows32(c, y)], s_o3[0], h == 1)
    for d in range(3):
        for i, (g, n, cond) in enumerate(gather_groups):
            send(both.at[pl.ds(g, n), rows32(c, y)], both.at[pl.ds(g, n), rows32(c, y)], s_n4[2 * d + i], d_y[d], cond)
    for i, (g, n, cond) in enumerate(gather_groups):
        send(both.at[pl.ds(g, n), rows32(c, y)], both.at[pl.ds(g, n), rows32(c, y)], s_n5[i], d_c, cond)

    for j in range(3):
        recv(low.at[j, quarter(x)], s_b2[j], odd)
        low_ring(j, lambda w: odd)
    for i in range(3):
        recv(ubuf.at[rem(y + 3 - i, 4), :, c], s_u2[i])
    send(ubuf.at[:, :, c], ubuf.at[:, :, c], s_u3[0], d_c)

    for i, (v, w) in enumerate(plane):
        src = rem(y + 4 - (i + 1) // 4, 4) * 4 + rem(x + 4 - (i + 1) % 4, 4)
        recv(obuf.at[src], s_c3[i], (c == 0) & jnp.logical_not(corner_dev))
    send(obuf, obuf, s_c4[0], d_c, c == 0)
    for d in range(3):
        src = rem(y + 3 - d, 4)
        for i, (g, n, cond) in enumerate(gather_groups):
            recv(both.at[pl.ds(g, n), rows32(c, src)], s_n4[2 * d + i], cond)
            send(both.at[pl.ds(g, n), rows32(c, src)], both.at[pl.ds(g, n), rows32(c, src)],
                 s_n5[2 * (d + 1) + i], d_c, cond)

    for i in range(3):
        recv(lbuf.at[pl.ds(rem(x + 3 - i, 4) * 8, 8)], s_l2[i])
    recv(ubuf.at[:, :, 1 - c], s_u3[0])
    for j in range(3):
        for i in range(3):
            recv(low.at[j, quarter(rem(x + 3 - i, 4))], s_b3[3 * j + i], jnp.logical_not(isq0))
    recv(obuf, s_c4[0], c == 1)
    for d in range(4):
        src = rem(y + 4 - d, 4)
        for i, (g, n, cond) in enumerate(gather_groups):
            recv(both.at[pl.ds(g, n), rows32(1 - c, src)], s_n5[2 * d + i], cond)
    for cond, d in pend:
        when(cond, d.wait_send)


def finish_kernel(ids, counts, piv, both, low, corner, l_t, u_inv, tiles, out, lower, upper):
    p = lax.axis_index("prow")
    q = lax.axis_index("pcol")
    block = pl.program_id(0)
    sub = lax.broadcasted_iota(jnp.int32, (SIDE, SIDE), 0)

    def hot_of(row):
        return piv[...] == (p + 16 * row) * SIDE + sub

    def swap(tile, row, old):
        hot = hot_of(row)
        moved = jnp.max(hot.astype(F32), axis=1, keepdims=True) > 0.5
        moved_rows = jnp.dot(hot.astype(BF), old, preferred_element_type=F32)
        return jnp.where(moved, moved_rows, tile.astype(F32))

    @pl.when(block == 0)
    def _():
        lt = l_t[...].astype(F32).reshape(SIDE, SIDE).astype(BF)
        u = u_inv[...].reshape(SIDE, SIDE)

        def step(k, carry):
            s = swap(low[k], ROW0 + k, corner[...].reshape(SIDE, SIDE)).astype(BF)
            lower[k] = jnp.dot(s, u, preferred_element_type=F32).astype(BF)
            upper[k] = lax.dot_general(
                lt, both[k], (((0,), (0,)), ((), ())), preferred_element_type=F32
            ).astype(BF)
            return carry

        lax.fori_loop(0, 3, step, 0)

    def slot_step(i, carry):
        s = block * 4 + i
        code = ids[0, 0, s]
        row, col = div(code, 8), rem(code, 8)
        live = s < counts[0, 0]
        low_row = row >= ROW0
        up_col = col >= COL0
        k = jnp.maximum(row - ROW0, 0)
        m = jnp.maximum(col - COL0, 0)
        trail = live & low_row & up_col
        top = live & (p == 0) & (row == 0) & up_col
        first = live & (q == 0) & (col == 0) & low_row
        diag = live & (p == 0) & (q == 0) & (code == 0)
        plain = live & jnp.logical_not(trail | top | first | diag)

        @pl.when(trail)
        def _():
            product = jnp.dot(lower[k], upper[m], preferred_element_type=F32)
            out[0, 0, i] = (swap(tiles[0, 0, i], row, both[3 + m]) - product).astype(BF)

        @pl.when(top)
        def _():
            out[0, 0, i] = upper[m]

        @pl.when(first)
        def _():
            out[0, 0, i] = lower[k]

        @pl.when(diag)
        def _():
            out[0, 0, i] = both[6]

        @pl.when(plain)
        def _():
            out[0, 0, i] = tiles[0, 0, i]

        @pl.when(jnp.logical_not(live))
        def _():
            out[0, 0, i] = jnp.zeros((SIDE, SIDE), BF)

        return carry

    lax.fori_loop(0, 4, slot_step, 0)


def body(tiles, tile_ids, counts, pivots, l_inverse, u_inverse):
    tile = (SIDE, SIDE)
    sds = jax.ShapeDtypeStruct
    vmem = pl.BlockSpec(memory_space=VM)
    smem = pl.BlockSpec(memory_space=pltpu.SMEM)
    hbm = pl.BlockSpec(memory_space=pltpu.HBM)
    dma = pltpu.SemaphoreType.DMA
    piv = pivots.reshape(1, SIDE)
    both, low, obuf, lbuf, ubuf = pl.pallas_call(
        exchange_kernel,
        out_shape=(
            sds((7, *tile), BF), sds((3, *tile), BF), sds((16, 16, SIDE), BF),
            sds((32, 8, SIDE), BF), sds((4, 2, 2, 16, SIDE), BF),
        ),
        in_specs=[smem, smem, vmem, hbm, hbm, hbm],
        out_specs=(vmem,) * 5,
        scratch_shapes=[
            VM((SLOTS, *tile), BF), VM((4, *tile), BF), VM((3, *tile), BF),
            VM((4, 128, SIDE), BF), VM((4, 128, SIDE), BF), VM((3, 4, 32, SIDE), BF),
            VM((4, 32, SIDE), BF), VM((4, 32, SIDE), BF), VM((3, 128, SIDE), BF),
            dma((190,)), dma((90,)), dma((3,)),
        ],
        compiler_params=pltpu.CompilerParams(
            collective_id=0, has_side_effects=True, vmem_limit_bytes=24 << 20),
        name="exchange",
    )(tile_ids, counts, piv, tiles, l_inverse.T, u_inverse)
    whole = lambda *shape: pl.BlockSpec(shape, lambda i: (0,) * len(shape), memory_space=VM)
    return pl.pallas_call(
        finish_kernel,
        grid=(4,),
        out_shape=sds((1, 1, SLOTS, *tile), BF),
        in_specs=[
            smem, smem, whole(1, SIDE), whole(7, *tile), whole(3, *tile), whole(16, 16, SIDE),
            whole(32, 8, SIDE), whole(16, 16, SIDE),
            pl.BlockSpec((1, 1, 4, *tile), lambda i: (0, 0, i, 0, 0), memory_space=VM),
        ],
        out_specs=pl.BlockSpec((1, 1, 4, *tile), lambda i: (0, 0, i, 0, 0), memory_space=VM),
        scratch_shapes=[VM((3, *tile), BF), VM((3, *tile), BF)],
        name="finish",
        compiler_params=pltpu.CompilerParams(vmem_limit_bytes=20 << 20),
    )(tile_ids, counts, piv, both, low, obuf, lbuf, ubuf.reshape(16, 16, SIDE), tiles)


def solution(mesh):
    return jax.shard_map(
        body,
        mesh=mesh,
        in_specs=(
            P("prow", "pcol", None, None, None), P("prow", "pcol", None), P("prow", "pcol"),
            P(), P(None, "pcol"), P("prow", None),
        ),
        out_specs=P("prow", "pcol", None, None, None),
        check_vma=False,
    )
```

time: 63.7 us -> 57.5 us (0.903)
  the two profiles are of different devices: /device:TPU:487 before, /device:TPU:1 now
where the time goes in v2:
time: 57.5 us; the launch traced here: 57.2 us
  Pallas kernels  52.3 us (91%)
  local copies, waits for them, and re-layouts  4.3 us (7%)
  between operations  0.67 us (1%)
    pallas_call x1, Pallas kernels, body(): pl.pallas_call(exchange_kernel, out_shape=(sds((7, *tile), BF), sds((3, *...  47.8 us
    pallas_call x1, Pallas kernels, body(): pl.pallas_call(finish_kernel, grid=(4,), out_shape=sds((1, 1, SLOTS, *til...  4.44 us
    unnamed x10, local copies, waits for them, and re-layouts  4.3 us

profile of v2, /device:TPU:1, one launch (start us, length us, event | category | flops | bytes accessed | tf_op | source)
XLA Modules:
  0.0 57.2 jit_solution(9546677043431088640)
XLA Ops:
  0.7 0.0 copy-start
  0.7 1.6 %copy-done = bf16[1,1,16,256,256]{4,3,2,1,0:T(8,128)(2,1)S(1)} copy-done((bf16[1,1,16,256,256]{4,3,2,1,0:T(8,128)(2,1)S(1)}, bf16[1,1,16,256,256]{4,3,2,1,0:T(8,128)(2,1)}, u32[]{:S(2)}) %copy-start) | copy-done | bytes 2097176
  2.2 0.0 copy-start.1
  2.2 0.7 %copy-done.1 = bf16[16,256]{1,0:T(8,128)(2,1)S(1)} copy-done((bf16[16,256]{1,0:T(8,128)(2,1)S(1)}, bf16[16,256]{1,0:T(8,128)(2,1)}, u32[]{:S(2)}) %copy-start.1) | copy-done | bytes 8216
  2.9 0.0 copy-start.2
  2.9 0.7 %copy-done.2 = bf16[256,8]{0,1:T(8,128)(2,1)S(1)} copy-done((bf16[256,8]{0,1:T(8,128)(2,1)S(1)}, bf16[256,8]{0,1:T(8,128)(2,1)}, u32[]{:S(2)}) %copy-start.2) | copy-done | bytes 4120
  3.6 0.0 copy-start.3
  3.6 0.7 %copy-done.3 = s32[256]{0:T(256)S(1)} copy-done((s32[256]{0:T(256)S(1)}, s32[256]{0:T(256)}, u32[]{:S(2)}) %copy-start.3) | copy-done | bytes 1048
  4.3 0.0 copy-start.4
  4.3 0.7 %copy-done.4 = s32[1,1,16]{2,1,0:T(1,128)S(1)} copy-done((s32[1,1,16]{2,1,0:T(1,128)S(1)}, s32[1,1,16]{2,1,0:T(1,128)}, u32[]{:S(2)}) %copy-start.4) | copy-done | bytes 88
  5.0 47.8 %exchange.1 = (bf16[7,256,256]{2,1,0:T(8,128)(2,1)S(1)}, bf16[3,256,256]{2,1,0:T(8,128)(2,1)S(1)}, bf16[16,16,256]{2,1,0:T(8,128)(2,1)S(1)}, bf16[32,8,256]{2,1,...) custom-call(s32[1,1,16]{2,1,0:T(1,128)S(1)} %copy-done.4, s32[1,1]{1,0:T(1,128)S(6)} %copy.7.counts, s32[1,256]{1,0:T(1,128)S(1)} %bitcast.5, ...), custom_call_target="tpu_custom_call" | custom-call | tf_op jit(solution)/shard_map/exchange/pallas_call | solution.py:384
  52.8 4.4 %finish.1 = bf16[1,1,16,256,256]{4,3,2,1,0:T(8,128)(2,1)} custom-call(s32[1,1,16]{2,1,0:T(1,128)S(1)} %copy-done.4, s32[1,1]{1,0:T(1,128)S(6)} %copy.7.counts, s32[1,256]{1,0:T(1,128)S(1)} %bitcast.6, bf16[7,256,256]{2,1,0:T(8,128)(2,1)S(1)} %get-tuple-element.10.both, bf16[3,256,256]{2,1,0:T(8,128)(2,1)S(1)} %get-tuple-element.11.low, ...), custom_call_target="tpu_custom_call" | custom-call | tf_op jit(solution)/shard_map/finish/pallas_call | solution.py:403
Async XLA Ops:
  0.7 1.6 %copy-start = (bf16[1,1,16,256,256]{4,3,2,1,0:T(8,128)(2,1)S(1)}, bf16[1,1,16,256,256]{4,3,2,1,0:T(8,128)(2,1)}, u32[]{:S(2)}) copy-start(bf16[1,1,16,256,256]{4,3,2,1,0:T(8,128)(2,1)} %tiles.1) | copy-start | bytes 6291460
  2.2 0.7 %copy-start.1 = (bf16[16,256]{1,0:T(8,128)(2,1)S(1)}, bf16[16,256]{1,0:T(8,128)(2,1)}, u32[]{:S(2)}) copy-start(bf16[16,256]{1,0:T(8,128)(2,1)} %u_part.1) | copy-start | bytes 24580
  2.9 0.7 %copy-start.2 = (bf16[256,8]{0,1:T(8,128)(2,1)S(1)}, bf16[256,8]{0,1:T(8,128)(2,1)}, u32[]{:S(2)}) copy-start(bf16[256,8]{0,1:T(8,128)(2,1)} %param.10) | copy-start | bytes 12292
  3.6 0.7 %copy-start.3 = (s32[256]{0:T(256)S(1)}, s32[256]{0:T(256)}, u32[]{:S(2)}) copy-start(s32[256]{0:T(256)} %param.9) | copy-start | bytes 3076
  4.3 0.7 %copy-start.4 = (s32[1,1,16]{2,1,0:T(1,128)S(1)}, s32[1,1,16]{2,1,0:T(1,128)}, u32[]{:S(2)}) copy-start(s32[1,1,16]{2,1,0:T(1,128)} %ids.3) | copy-start | bytes 196

commit v3 on v2

v3 whole, which is shorter than its diff:
```python
import jax
import jax.numpy as jnp
from jax import lax
from jax.experimental import pallas as pl
from jax.experimental.pallas import tpu as pltpu
from jax.sharding import PartitionSpec as P

MESH = pl.DeviceIdType.MESH
SIDE = 256
SLOTS = 16
ROW0 = 13
COL0 = 5
BF = jnp.bfloat16
F32 = jnp.float32
VM = pltpu.VMEM
EXCHANGE_VMEM = 24 << 20


def div(a, b):
    return lax.div(a, jnp.int32(b))


def rem(a, b):
    return lax.rem(a, jnp.int32(b))


TREE = [(4, 0), (2, 0), (1, 0), (6, 4), (5, 4), (3, 2), (7, 6)]
ROWS = (0, ROW0, ROW0 + 1, ROW0 + 2)
COLS = (COL0, COL0 + 1, COL0 + 2, 0)


def exchange_kernel(
    ids_hbm, counts, piv_hbm, tiles_hbm, l_part, u_part,
    both, low, obuf, lbuf, ubuf, tiles, piv,
    newp, r1, a1, r2, a2, r3, r4, m4, m5, r5, owner, chips, ids, ssem, rsem, lsem,
):
    p = lax.axis_index("prow")
    q = lax.axis_index("pcol")
    y, h, c = div(p, 4), rem(div(p, 2), 2), rem(p, 2)
    x, z = div(q, 8), rem(q, 8)
    isq0 = q == 0
    isp0 = p == 0
    corner_dev = isq0 & isp0

    get_tiles = pltpu.make_async_copy(tiles_hbm.at[0, 0], tiles, lsem.at[0])
    get_l = pltpu.make_async_copy(l_part, lbuf.at[q], lsem.at[1])
    get_u = pltpu.make_async_copy(u_part, ubuf.at[y, h, c], lsem.at[2])
    get_ids = pltpu.make_async_copy(ids_hbm, ids, lsem.at[3])
    get_piv = pltpu.make_async_copy(piv_hbm, piv, lsem.at[4])
    get_ids.start()
    get_piv.start()
    get_tiles.start()
    get_l.start()
    get_u.start()

    def P_(yy, hh, cc):
        return yy * 4 + hh * 2 + cc

    ys = [rem(y + d, 4) for d in (1, 2, 3)]
    xs = [rem(x + d, 4) for d in (1, 2, 3)]
    d_y = [(P_(v, h, c), q) for v in ys]
    d_h = (P_(y, 1 - h, c), q)
    d_c = (P_(y, h, 1 - c), q)
    d_x = [(p, v * 8 + z) for v in xs]
    d_z = [(p, x * 8 + rem(z + d, 8)) for d in range(1, 8)]
    plane = [(rem(y + k // 4, 4), rem(x + k % 4, 4)) for k in range(1, 16)]
    d_plane = [(P_(v, h, c), w * 8 + z) for v, w in plane]
    d_ring = [(P_(y, rem(h + k // 8, 2), c), x * 8 + rem(z + k % 8, 8)) for k in range(1, 16)]

    bar = pltpu.get_barrier_semaphore()
    greet = d_plane + d_ring + [d_c]
    for dev in greet:
        pl.semaphore_signal(bar, inc=1, device_id=dev, device_id_type=MESH)

    get_ids.wait()

    def look(s, found):
        code = jnp.where(s < counts[0, 0], ids[0, 0, s], -1)
        return tuple(
            jnp.where(code == ROWS[i // 4] * 8 + COLS[i % 4], s, f) for i, f in enumerate(found)
        )

    slots = lax.fori_loop(0, SLOTS, look, (jnp.int32(-1),) * 16)

    def tile_at(i, j):
        slot = slots[4 * i + j]
        tile = tiles[jnp.maximum(slot, 0)]
        return jnp.where(slot >= 0, tile, jnp.zeros_like(tile))

    sub = lax.broadcasted_iota(jnp.int32, (SIDE, SIDE), 0)
    lane = lax.broadcasted_iota(jnp.int32, (SIDE, SIDE), 1)
    get_piv.wait()
    wanted = jnp.sum(jnp.where(sub == lane, piv[...].astype(F32), 0.0), axis=1, keepdims=True)
    trow = jnp.floor(wanted * (1.0 / SIDE))
    holder = trow - 16.0 * jnp.floor(trow * (1.0 / 16))
    chip = jnp.floor(holder * 0.5)
    owner[...] = jnp.broadcast_to(holder, (SIDE, SIDE)).astype(BF)
    chips[...] = jnp.broadcast_to(chip, (SIDE, SIDE)).astype(BF)
    hots = [
        (wanted == ((p + 16 * r) * SIDE + lane).astype(F32)).astype(F32) for r in ROWS
    ]
    given = (isp0 & (holder > 0.5)).astype(F32)
    hots[0] = given * (sub == lane).astype(F32) + (1.0 - given) * hots[0]
    hots = [hot.astype(BF) for hot in hots]
    get_tiles.wait()

    def new_column(m):
        acc = jnp.dot(hots[0], tile_at(0, m), preferred_element_type=F32)
        for i in range(1, 4):
            acc += jnp.dot(hots[i], tile_at(i, m), preferred_element_type=F32)
        newp[m] = acc.astype(BF)

    for m in range(3):
        new_column(m)

    @pl.when(isq0)
    def _():
        new_column(3)
        for k in range(3):
            low[k] = tile_at(1 + k, 3)

    @pl.when(corner_dev)
    def _():
        obuf[...] = tile_at(0, 3).reshape(16, 16, SIDE)

    pl.semaphore_wait(bar, len(greet))

    pend = []
    counter = [0, 0]

    def when(cond, fn):
        if cond is None:
            fn()
        else:
            pl.when(cond)(fn)

    def sems(n):
        base = counter[1]
        counter[1] += n
        return [rsem.at[base + i] for i in range(n)]

    def send(src, dst, rs, dev, cond=None):
        d = pltpu.make_async_remote_copy(
            src_ref=src, dst_ref=dst, send_sem=ssem.at[counter[0]], recv_sem=rs,
            device_id=dev, device_id_type=MESH)
        counter[0] += 1
        when(cond, d.start)
        pend.append((cond, d))

    def recv(dst, rs, cond=None):
        d = pltpu.make_async_remote_copy(
            src_ref=dst, dst_ref=dst, send_sem=ssem.at[0], recv_sem=rs,
            device_id=d_c, device_id_type=MESH)
        when(cond, d.wait_recv)

    def al(v, n):
        return pl.multiple_of(v, n)

    def rows32(cc, yy):
        return pl.ds(al(cc * 128 + yy * 32, 32), 32)

    def quarter(v):
        return pl.ds(al(v * 64, 64), 64)

    s_n1, s_n2, s_n3, s_n4, s_n5 = sems(4), sems(12), sems(4), sems(12), sems(4)
    s_b1, s_b2, s_b3 = sems(3), sems(3), sems(9)
    s_c1, s_c2, s_c3, s_c4 = sems(1), sems(1), sems(15), sems(1)
    s_l1, s_l2 = sems(7), sems(3)
    s_u1, s_u2, s_u3 = sems(1), sems(3), sems(1)
    cols = [(0, None), (1, None), (2, None), (3, isq0)]
    my_half, its_half = pl.ds(al(c * 128, 128), 128), pl.ds(al((1 - c) * 128, 128), 128)
    my_rows = rows32(c, y)
    my_chip = y * 2 + h

    def is_(ref, rows, value):
        return ref[rows] == jnp.full((1, 1), value, F32).astype(BF)

    def run(cond, fn):
        if cond is None:
            fn()
        else:
            pl.when(cond)(fn)

    for m, cond in cols:
        send(newp.at[m, its_half], r1.at[m], s_n1[m], d_c, cond)
    mine = y * 4 + x
    for i, (v, w) in enumerate(plane):
        send(obuf.at[v * 4 + w], obuf.at[v * 4 + w], s_c1[0], d_plane[i], corner_dev)
    source = (z == 0) & (h == 0) & (c == 0)
    for dev in d_ring:
        send(obuf.at[mine], obuf.at[mine], s_c2[0], dev, corner_dev)
    get_u.wait()
    send(ubuf.at[y, h, c], ubuf.at[y, h, c], s_u1[0], d_h)
    get_l.wait()
    for i in range(7):
        send(lbuf.at[q], lbuf.at[q], s_l1[i], d_z[i])
    for j in range(3):
        for i in range(3):
            send(low.at[j, quarter(xs[i])], low.at[j, quarter(xs[i])], s_b1[j], d_x[i], isq0)

    def low_tree(j, parent, cond):
        for child, par in TREE:
            if par == parent:
                send(low.at[j, quarter(x)], low.at[j, quarter(x)], s_b2[j], (p, x * 8 + child), cond)

    def low_ring(j, cond):
        for i in range(3):
            send(low.at[j, quarter(x)], low.at[j, quarter(x)], s_b3[3 * j + i], d_x[i], cond(xs[i]))

    for j in range(3):
        low_tree(j, 0, isq0)

    for m, cond in cols:
        recv(r1.at[m], s_n1[m], cond)

        def chip_rows(m=m):
            own, other = newp[m, my_half], r1[m]
            odd_one = is_(owner, my_half, p + 1 - c)
            keep = jnp.where(c == 0, own, other)
            a1[m] = jnp.where(odd_one, jnp.where(c == 0, other, own), keep)

        run(cond, chip_rows)
        for d in range(3):
            send(a1.at[m, pl.ds(al(ys[d] * 32, 32), 32)], r2.at[m, d], s_n2[3 * m + d], d_y[d], cond)

    relay = source & jnp.logical_not(corner_dev)
    recv(obuf.at[mine], s_c1[0], relay)
    for dev in d_ring:
        send(obuf.at[mine], obuf.at[mine], s_c2[0], dev, relay)
    second = (x > 0) & (z == 0)
    for j in range(3):
        recv(low.at[j, quarter(x)], s_b1[j], second)
        low_tree(j, 0, second)
    for j in range(3):
        low_ring(j, lambda w: (z == 0) & (w > 0))

    for m, cond in cols:
        for d in range(3):
            recv(r2.at[m, d], s_n2[3 * m + d], cond)

        def half_rows(m=m):
            own = a1[m, pl.ds(al(y * 32, 32), 32)]
            got = [r2[m, d] for d in range(3)]
            first = own
            rest = jnp.zeros_like(own)
            for d in range(3):
                at0 = ys[2 - d] == 0
                first = jnp.where(at0, got[d], first)
                rest = rest + jnp.where(at0, own, got[d])
            rest = jnp.where(y == 0, got[0] + got[1] + got[2], rest)
            here = is_(chips, my_rows, 2 + h) | is_(chips, my_rows, 4 + h) | is_(chips, my_rows, 6 + h)
            a2[m, 0] = jnp.where(here, rest, first)
            a2[m, 1] = first

        run(cond, half_rows)
        send(a2.at[m, 0], r3.at[m], s_n3[m], d_h, cond)

    for i in range(7):
        recv(lbuf.at[q], s_l1[i])
    for i in range(3):
        send(lbuf.at[pl.ds(x * 8, 8)], lbuf.at[pl.ds(x * 8, 8)], s_l2[i], d_x[i])
    recv(ubuf.at[y, h, c], s_u1[0])
    for i in range(3):
        send(ubuf.at[y, :, c], ubuf.at[y, :, c], s_u2[i], d_y[i])
    odd = rem(z, 2) == 1
    even = (z > 0) & (rem(z, 2) == 0)
    for j in range(3):
        recv(low.at[j, quarter(x)], s_b2[j], even)
        for parent in (4, 2, 6):
            low_tree(j, parent, z == parent)
    for j in range(3):
        low_ring(j, lambda w: even)

    recv(obuf.at[mine], s_c2[0], (c == 0) & jnp.logical_not(source))
    for i, (v, w) in enumerate(plane):
        send(obuf.at[mine], obuf.at[mine], s_c3[i], d_plane[i],
             (c == 0) & jnp.logical_not((z == 0) & (h == 0) & (v == 0) & (w == 0)))

    for m, cond in cols:
        recv(r3.at[m], s_n3[m], cond)

        def all_rows(m=m):
            mine_, theirs = a2[m, 0], r3[m]
            here = is_(chips, my_rows, h) | is_(chips, my_rows, 2 + h)
            here = here | is_(chips, my_rows, 4 + h) | is_(chips, my_rows, 6 + h)
            new = jnp.where(here, mine_, theirs)
            old = jnp.where(h == 0, a2[m, 1], theirs)
            for d in range(3):
                m4[m, d] = jnp.where(is_(chips, my_rows, ys[d] * 2 + h), old, new)
            r4[m, pl.ds(al(y * 32, 32), 32)] = jnp.where(is_(chips, my_rows, my_chip), old, new)

        run(cond, all_rows)
        for d in range(3):
            send(m4.at[m, d], r4.at[m, pl.ds(al(y * 32, 32), 32)], s_n4[3 * m + d], d_y[d], cond)

    for j in range(3):
        recv(low.at[j, quarter(x)], s_b2[j], odd)
        low_ring(j, lambda w: odd)
    for i in range(3):
        recv(ubuf.at[rem(y + 3 - i, 4), :, c], s_u2[i])
    send(ubuf.at[:, :, c], ubuf.at[:, :, c], s_u3[0], d_c)

    for i, (v, w) in enumerate(plane):
        src = rem(y + 4 - (i + 1) // 4, 4) * 4 + rem(x + 4 - (i + 1) % 4, 4)
        recv(obuf.at[src], s_c3[i], (c == 0) & jnp.logical_not(corner_dev))
    send(obuf, obuf, s_c4[0], d_c, c == 0)
    for m, cond in cols:
        for d in range(3):
            recv(r4.at[m, pl.ds(al(rem(y + 3 - d, 4) * 32, 32), 32)], s_n4[3 * m + d], cond)

        def core_rows(m=m):
            got, chip_ = r4[m], a1[m]
            here = is_(chips, my_half, my_chip)
            new = jnp.where(here, chip_, got)
            own, other = newp[m, my_half], r1[m]
            old = jnp.where(my_chip == 0, jnp.where(c == 0, own, other), got)
            m5[m] = jnp.where(is_(owner, my_half, p + 1 - 2 * c), old, new)
            if m < 3:
                both[m, my_half] = new
                both[3 + m, my_half] = old
            else:
                both[6, my_half] = new

        run(cond, core_rows)
        send(m5.at[m], r5.at[m], s_n5[m], d_c, cond)

    for i in range(3):
        recv(lbuf.at[pl.ds(rem(x + 3 - i, 4) * 8, 8)], s_l2[i])
    recv(ubuf.at[:, :, 1 - c], s_u3[0])
    for j in range(3):
        for i in range(3):
            recv(low.at[j, quarter(rem(x + 3 - i, 4))], s_b3[3 * j + i], jnp.logical_not(isq0))
    recv(obuf, s_c4[0], c == 1)
    for m, cond in cols:
        recv(r5.at[m], s_n5[m], cond)

        def last_rows(m=m):
            got = r5[m]
            new = jnp.where(is_(owner, its_half, p), newp[m, its_half], got)
            if m < 3:
                both[m, its_half] = new
                both[3 + m, its_half] = got
            else:
                both[6, its_half] = new

        run(cond, last_rows)

    @pl.when(isp0)
    def _():
        for m in range(3):
            both[3 + m] = tile_at(0, m)

    for cond, d in pend:
        when(cond, d.wait_send)


def finish_kernel(
    ids_hbm, counts, piv, both, low, corner, l_t, u_inv, tiles, out,
    done, lower, upper, ids, sems,
):
    get_ids = pltpu.make_async_copy(ids_hbm, ids, sems.at[SLOTS])
    get_ids.start()
    p = lax.axis_index("prow")
    q = lax.axis_index("pcol")
    sub = lax.broadcasted_iota(jnp.int32, (SIDE, SIDE), 0)

    def hot_of(row):
        return piv[...] == (p + 16 * row) * SIDE + sub

    def swap(tile, row, old):
        hot = hot_of(row)
        moved = jnp.max(hot.astype(F32), axis=1, keepdims=True) > 0.5
        moved_rows = jnp.dot(hot.astype(BF), old, preferred_element_type=F32)
        return jnp.where(moved, moved_rows, tile.astype(F32))

    def kind(s):
        code = ids[0, 0, s]
        row, col = div(code, 8), rem(code, 8)
        live = s < counts[0, 0]
        low_row = row >= ROW0
        up_col = col >= COL0
        trail = live & low_row & up_col
        top = live & (p == 0) & (row == 0) & up_col
        first = live & (q == 0) & (col == 0) & low_row
        diag = live & (p == 0) & (q == 0) & (code == 0)
        plain = live & jnp.logical_not(trail | top | first | diag)
        k = jnp.maximum(row - ROW0, 0)
        m = jnp.maximum(col - COL0, 0)
        return live, trail, top, first, diag, plain, row, k, m

    def put(src, s):
        return pltpu.make_async_copy(src.at[s], out.at[0, 0, s], sems.at[s])

    def untouched(s, carry):
        live, trail, top, first, diag, plain, row, k, m = kind(s)

        @pl.when(plain)
        def _():
            put(tiles, s).start()

        @pl.when(jnp.logical_not(live))
        def _():
            done[s] = jnp.zeros((SIDE, SIDE), BF)
            put(done, s).start()

        return carry

    lt = l_t[...].astype(F32).reshape(SIDE, SIDE).astype(BF)
    u = u_inv[...].reshape(SIDE, SIDE)

    def solve(k, carry):
        s = swap(low[k], ROW0 + k, corner[...].reshape(SIDE, SIDE)).astype(BF)
        lower[k] = jnp.dot(s, u, preferred_element_type=F32).astype(BF)
        upper[k] = lax.dot_general(
            lt, both[k], (((0,), (0,)), ((), ())), preferred_element_type=F32
        ).astype(BF)
        return carry

    solve(0, 0)
    get_ids.wait()
    lax.fori_loop(0, SLOTS, untouched, 0)
    lax.fori_loop(1, 3, solve, 0)

    def touched(s, carry):
        live, trail, top, first, diag, plain, row, k, m = kind(s)

        @pl.when(trail)
        def _():
            product = jnp.dot(lower[k], upper[m], preferred_element_type=F32)
            done[s] = (swap(tiles[s], row, both[3 + m]) - product).astype(BF)

        @pl.when(top)
        def _():
            done[s] = upper[m]

        @pl.when(first)
        def _():
            done[s] = lower[k]

        @pl.when(diag)
        def _():
            done[s] = both[6]

        @pl.when(trail | top | first | diag)
        def _():
            put(done, s).start()

        return carry

    lax.fori_loop(0, SLOTS, touched, 0)

    def wait(s, carry):
        put(done, s).wait()
        return carry

    lax.fori_loop(0, SLOTS, wait, 0)


def body(tiles, tile_ids, counts, pivots, l_inverse, u_inverse):
    tile = (SIDE, SIDE)
    sds = jax.ShapeDtypeStruct
    vmem = pl.BlockSpec(memory_space=VM)
    smem = pl.BlockSpec(memory_space=pltpu.SMEM)
    hbm = pl.BlockSpec(memory_space=pltpu.HBM)
    dma = pltpu.SemaphoreType.DMA

    def stay(v):
        return pltpu.with_memory_space_constraint(v, pltpu.HBM)

    both, low, obuf, lbuf, ubuf, held, piv = pl.pallas_call(
        exchange_kernel,
        out_shape=(
            sds((7, *tile), BF), sds((3, *tile), BF), sds((16, 16, SIDE), BF),
            sds((32, 8, SIDE), BF), sds((4, 2, 2, 16, SIDE), BF), sds((SLOTS, *tile), BF),
            sds((1, SIDE), jnp.int32),
        ),
        in_specs=[hbm, smem] + [hbm] * 4,
        out_specs=(vmem,) * 7,
        scratch_shapes=[
            VM((4, *tile), BF), VM((4, 128, SIDE), BF), VM((4, 128, SIDE), BF),
            VM((4, 3, 32, SIDE), BF), VM((4, 2, 32, SIDE), BF), VM((4, 32, SIDE), BF),
            VM((4, 128, SIDE), BF), VM((4, 3, 32, SIDE), BF), VM((4, 128, SIDE), BF),
            VM((4, 128, SIDE), BF), VM(tile, BF), VM(tile, BF),
            pltpu.SMEM((1, 1, SLOTS), jnp.int32),
            dma((190,)), dma((90,)), dma((5,)),
        ],
        compiler_params=pltpu.CompilerParams(
            collective_id=0, has_side_effects=True, vmem_limit_bytes=EXCHANGE_VMEM),
        name="exchange",
    )(stay(tile_ids), counts, stay(pivots.reshape(1, SIDE)), stay(tiles), stay(l_inverse.T), stay(u_inverse))
    return pl.pallas_call(
        finish_kernel,
        out_shape=sds((1, 1, SLOTS, *tile), BF),
        in_specs=[hbm, smem] + [vmem] * 7,
        out_specs=hbm,
        scratch_shapes=[
            VM((SLOTS, *tile), BF), VM((3, *tile), BF), VM((3, *tile), BF),
            pltpu.SMEM((1, 1, SLOTS), jnp.int32), dma((SLOTS + 1,)),
        ],
        compiler_params=pltpu.CompilerParams(vmem_limit_bytes=20 << 20),
        name="finish",
    )(stay(tile_ids), counts, piv, both, low, obuf, lbuf, ubuf.reshape(16, 16, SIDE), held)


def solution(mesh):
    return jax.shard_map(
        body,
        mesh=mesh,
        in_specs=(
            P("prow", "pcol", None, None, None), P("prow", "pcol", None), P("prow", "pcol"),
            P(), P(None, "pcol"), P("prow", None),
        ),
        out_specs=P("prow", "pcol", None, None, None),
        check_vma=False,
    )
```

time: 57.5 us -> 47.1 us (0.82)
  Pallas kernels: 52.3 us -> 45.7 us
  local copies, waits for them, and re-layouts: 4.3 us -> 0 us
    pallas_call x1, Pallas kernels: 47.8 us -> 41.3 us  [body(): pl.pallas_call(exchange_kernel, out_shape=(sds((7, *tile), BF), sds((3, *...]
    unnamed x10 -> x0, local copies, waits for them, and re-layouts: 4.3 us -> none
where the time goes in v3:
time: 47.1 us; the launch traced here: 46.4 us
  Pallas kernels  45.7 us (97%)
  between operations  0.66 us (1%)
    pallas_call x1, Pallas kernels, body(): pl.pallas_call(exchange_kernel, out_shape=(sds((7, *tile), BF), sds((3, *...  41.3 us
    pallas_call x1, Pallas kernels, body(): pl.pallas_call(finish_kernel, out_shape=sds((1, 1, SLOTS, *tile), BF), in...  4.4 us

profile of v3, /device:TPU:1, one launch (start us, length us, event | category | flops | bytes accessed | tf_op | source)
XLA Modules:
  0.0 46.4 jit_solution(7275739673360923816)
XLA Ops:
  0.7 41.3 %exchange.1 = (bf16[7,256,256]{2,1,0:T(8,128)(2,1)S(1)}, bf16[3,256,256]{2,1,0:T(8,128)(2,1)S(1)}, bf16[16,16,256]{2,1,0:T(8,128)(2,1)S(1)}, bf16[32,8,256]{2,1,...) custom-call(s32[1,1,16]{2,1,0:T(1,128)} %ids_hbm.3, ...), custom_call_target="tpu_custom_call" | custom-call | tf_op jit(solution)/shard_map/exchange/pallas_call | solution.py:470
  42.0 4.4 %finish.1 = bf16[1,1,16,256,256]{4,3,2,1,0:T(8,128)(2,1)} custom-call(s32[1,1,16]{2,1,0:T(1,128)} %ids_hbm.3, s32[1,1]{1,0:T(1,128)S(6)} %copy.7.counts, s32[1,256]{1,0:T(1,128)S(1)} %get-tuple-element.12.piv, bf16[7,256,256]{2,1,0:T(8,128)(2,1)S(1)} %get-tuple-element.13.both, bf16[3,256,256]{2,1,0:T(8,128)(2,1)S(1)} %get-tuple-element.14.low, ...), custom_call_target="tpu_custom_call" | custom-call | tf_op jit(solution)/shard_map/finish/pallas_call | solution.py:491

commit v4 on v3

--- a/solution.py
+++ b/solution.py
@@ -24,15 +24,15 @@
     return lax.rem(a, jnp.int32(b))
 
 
-TREE = [(4, 0), (2, 0), (1, 0), (6, 4), (5, 4), (3, 2), (7, 6)]
+TREE = [(3, 0), (1, 0), (2, 1), (5, 3), (4, 3), (7, 5), (6, 5)]
 ROWS = (0, ROW0, ROW0 + 1, ROW0 + 2)
 COLS = (COL0, COL0 + 1, COL0 + 2, 0)
 
 
 def exchange_kernel(
     ids_hbm, counts, piv_hbm, tiles_hbm, l_part, u_part,
-    both, low, obuf, lbuf, ubuf, tiles, piv,
-    newp, r1, a1, r2, a2, r3, r4, m4, m5, r5, owner, chips, ids, ssem, rsem, lsem,
+    both, low, obuf, lbuf, ubuf, tiles, hot_out, keep_out,
+    newp, r1, a1, r2, a2, r3, r4, m4, m5, r5, owner, chips, ids, piv, ssem, rsem, lsem,
 ):
     p = lax.axis_index("prow")
     q = lax.axis_index("pcol")
@@ -210,6 +210,12 @@
     for j in range(3):
         low_tree(j, 0, isq0)
 
+    for k in range(3):
+        takes = (piv[...] == (p + 16 * ROWS[k + 1]) * SIDE + sub).astype(F32)
+        stays = 1.0 - jnp.max(takes, axis=1, keepdims=True)
+        hot_out[k] = takes.astype(BF)
+        keep_out[k] = jnp.broadcast_to(stays, (SIDE, SIDE)).astype(BF)
+
     for m, cond in cols:
         recv(r1.at[m], s_n1[m], cond)
 
@@ -262,11 +268,11 @@
     recv(ubuf.at[y, h, c], s_u1[0])
     for i in range(3):
         send(ubuf.at[y, :, c], ubuf.at[y, :, c], s_u2[i], d_y[i])
-    odd = rem(z, 2) == 1
-    even = (z > 0) & (rem(z, 2) == 0)
+    even = (z == 1) | (z == 3) | (z == 5)
+    odd = (z > 0) & jnp.logical_not(even)
     for j in range(3):
         recv(low.at[j, quarter(x)], s_b2[j], even)
-        for parent in (4, 2, 6):
+        for parent in (1, 3, 5):
             low_tree(j, parent, z == parent)
     for j in range(3):
         low_ring(j, lambda w: even)
@@ -355,23 +361,17 @@
 
 
 def finish_kernel(
-    ids_hbm, counts, piv, both, low, corner, l_t, u_inv, tiles, out,
+    ids_hbm, counts, hot, keep, both, low, corner, l_t, u_inv, tiles, out,
     done, lower, upper, ids, sems,
 ):
     get_ids = pltpu.make_async_copy(ids_hbm, ids, sems.at[SLOTS])
     get_ids.start()
     p = lax.axis_index("prow")
     q = lax.axis_index("pcol")
-    sub = lax.broadcasted_iota(jnp.int32, (SIDE, SIDE), 0)
-
-    def hot_of(row):
-        return piv[...] == (p + 16 * row) * SIDE + sub
-
-    def swap(tile, row, old):
-        hot = hot_of(row)
-        moved = jnp.max(hot.astype(F32), axis=1, keepdims=True) > 0.5
-        moved_rows = jnp.dot(hot.astype(BF), old, preferred_element_type=F32)
-        return jnp.where(moved, moved_rows, tile.astype(F32))
+
+    def swap(tile, k, old):
+        moved = jnp.dot(hot[k], old, preferred_element_type=F32)
+        return (tile * keep[k]).astype(F32) + moved
 
     def kind(s):
         code = ids[0, 0, s]
@@ -405,15 +405,13 @@
 
         return carry
 
-    lt = l_t[...].astype(F32).reshape(SIDE, SIDE).astype(BF)
+    left = jnp.transpose(l_t[...].astype(F32).reshape(SIDE, SIDE)).astype(BF)
     u = u_inv[...].reshape(SIDE, SIDE)
 
     def solve(k, carry):
-        s = swap(low[k], ROW0 + k, corner[...].reshape(SIDE, SIDE)).astype(BF)
+        s = swap(low[k], k, corner[...].reshape(SIDE, SIDE)).astype(BF)
         lower[k] = jnp.dot(s, u, preferred_element_type=F32).astype(BF)
-        upper[k] = lax.dot_general(
-            lt, both[k], (((0,), (0,)), ((), ())), preferred_element_type=F32
-        ).astype(BF)
+        upper[k] = jnp.dot(left, both[k], preferred_element_type=F32).astype(BF)
         return carry
 
     solve(0, 0)
@@ -427,7 +425,7 @@
         @pl.when(trail)
         def _():
             product = jnp.dot(lower[k], upper[m], preferred_element_type=F32)
-            done[s] = (swap(tiles[s], row, both[3 + m]) - product).astype(BF)
+            done[s] = (swap(tiles[s], k, both[3 + m]) - product).astype(BF)
 
         @pl.when(top)
         def _():
@@ -467,21 +465,21 @@
     def stay(v):
         return pltpu.with_memory_space_constraint(v, pltpu.HBM)
 
-    both, low, obuf, lbuf, ubuf, held, piv = pl.pallas_call(
+    both, low, obuf, lbuf, ubuf, held, hot, keep = pl.pallas_call(
         exchange_kernel,
         out_shape=(
             sds((7, *tile), BF), sds((3, *tile), BF), sds((16, 16, SIDE), BF),
             sds((32, 8, SIDE), BF), sds((4, 2, 2, 16, SIDE), BF), sds((SLOTS, *tile), BF),
-            sds((1, SIDE), jnp.int32),
+            sds((3, *tile), BF), sds((3, *tile), BF),
         ),
         in_specs=[hbm, smem] + [hbm] * 4,
-        out_specs=(vmem,) * 7,
+        out_specs=(vmem,) * 8,
         scratch_shapes=[
             VM((4, *tile), BF), VM((4, 128, SIDE), BF), VM((4, 128, SIDE), BF),
             VM((4, 3, 32, SIDE), BF), VM((4, 2, 32, SIDE), BF), VM((4, 32, SIDE), BF),
             VM((4, 128, SIDE), BF), VM((4, 3, 32, SIDE), BF), VM((4, 128, SIDE), BF),
             VM((4, 128, SIDE), BF), VM(tile, BF), VM(tile, BF),
-            pltpu.SMEM((1, 1, SLOTS), jnp.int32),
+            pltpu.SMEM((1, 1, SLOTS), jnp.int32), VM((1, SIDE), jnp.int32),
             dma((190,)), dma((90,)), dma((5,)),
         ],
         compiler_params=pltpu.CompilerParams(
@@ -491,7 +489,7 @@
     return pl.pallas_call(
         finish_kernel,
         out_shape=sds((1, 1, SLOTS, *tile), BF),
-        in_specs=[hbm, smem] + [vmem] * 7,
+        in_specs=[hbm, smem] + [vmem] * 8,
         out_specs=hbm,
         scratch_shapes=[
             VM((SLOTS, *tile), BF), VM((3, *tile), BF), VM((3, *tile), BF),
@@ -499,7 +497,7 @@
         ],
         compiler_params=pltpu.CompilerParams(vmem_limit_bytes=20 << 20),
         name="finish",
-    )(stay(tile_ids), counts, piv, both, low, obuf, lbuf, ubuf.reshape(16, 16, SIDE), held)
+    )(stay(tile_ids), counts, hot, keep, both, low, obuf, lbuf, ubuf.reshape(16, 16, SIDE), held)
 
 
 def solution(mesh):

time: 47.1 us -> 46.4 us (0.985)
  the two profiles are of different devices: /device:TPU:1 before, /device:TPU:161 now
where the time goes in v4:
time: 46.4 us; the launch traced here: 46.3 us
  Pallas kernels  45.6 us (98%)
  between operations  0.66 us (1%)
    pallas_call x1, Pallas kernels, body(): pl.pallas_call(exchange_kernel, out_shape=(sds((7, *tile), BF), sds((3, *...  41.4 us
    pallas_call x1, Pallas kernels, body(): pl.pallas_call(finish_kernel, out_shape=sds((1, 1, SLOTS, *tile), BF), in...  4.23 us

profile of v4, /device:TPU:161, one launch (start us, length us, event | category | flops | bytes accessed | tf_op | source)
XLA Modules:
  0.0 46.3 jit_solution(12981286263819741224)
XLA Ops:
  0.7 41.4 %exchange.1 = (bf16[7,256,256]{2,1,0:T(8,128)(2,1)S(1)}, bf16[3,256,256]{2,1,0:T(8,128)(2,1)S(1)}, bf16[16,16,256]{2,1,0:T(8,128)(2,1)S(1)}, bf16[32,8,256]{2,1,...) custom-call(s32[1,1,16]{2,1,0:T(1,128)} %ids_hbm.3, ...), custom_call_target="tpu_custom_call" | custom-call | tf_op jit(solution)/shard_map/exchange/pallas_call | solution.py:468
  42.1 4.2 %finish.1 = bf16[1,1,16,256,256]{4,3,2,1,0:T(8,128)(2,1)} custom-call(s32[1,1,16]{2,1,0:T(1,128)} %ids_hbm.3, s32[1,1]{1,0:T(1,128)S(6)} %copy.7.counts, bf16[3,256,256]{2,1,0:T(8,128)(2,1)S(1)} %get-tuple-element.13.hot, bf16[3,256,256]{2,1,0:T(8,128)(2,1)S(1)} %get-tuple-element.14.keep, bf16[7,256,256]{2,1,0:T(8,128)(2,1)S(1)} %get-tuple-element.15.both, ...), custom_call_target="tpu_custom_call" | custom-call | tf_op jit(solution)/shard_map/finish/pallas_call | solution.py:489

commit v5 on v4

--- a/solution.py
+++ b/solution.py
@@ -24,7 +24,7 @@
     return lax.rem(a, jnp.int32(b))
 
 
-TREE = [(3, 0), (1, 0), (2, 1), (5, 3), (4, 3), (7, 5), (6, 5)]
+TREE = [(4, 0), (1, 0), (6, 4), (3, 4), (2, 1), (7, 6), (5, 6)]
 ROWS = (0, ROW0, ROW0 + 1, ROW0 + 2)
 COLS = (COL0, COL0 + 1, COL0 + 2, 0)
 
@@ -268,11 +268,11 @@
     recv(ubuf.at[y, h, c], s_u1[0])
     for i in range(3):
         send(ubuf.at[y, :, c], ubuf.at[y, :, c], s_u2[i], d_y[i])
-    even = (z == 1) | (z == 3) | (z == 5)
+    even = (z == 1) | (z == 4) | (z == 6)
     odd = (z > 0) & jnp.logical_not(even)
     for j in range(3):
         recv(low.at[j, quarter(x)], s_b2[j], even)
-        for parent in (1, 3, 5):
+        for parent in (1, 4, 6):
             low_tree(j, parent, z == parent)
     for j in range(3):
         low_ring(j, lambda w: even)

time: 46.4 us -> 45.6 us (0.983)
  the two profiles are of different devices: /device:TPU:161 before, /device:TPU:33 now
where the time goes in v5:
time: 45.6 us; the launch traced here: 45.7 us
  Pallas kernels  45.1 us (99%)
  between operations  0.66 us (1%)
    pallas_call x1, Pallas kernels, body(): pl.pallas_call(exchange_kernel, out_shape=(sds((7, *tile), BF), sds((3, *...  41 us
    pallas_call x1, Pallas kernels, body(): pl.pallas_call(finish_kernel, out_shape=sds((1, 1, SLOTS, *tile), BF), in...  4.06 us

profile of v5, /device:TPU:33, one launch (start us, length us, event | category | flops | bytes accessed | tf_op | source)
XLA Modules:
  0.0 45.7 jit_solution(13813751474112406966)
XLA Ops:
  0.7 41.0 %exchange.1 = (bf16[7,256,256]{2,1,0:T(8,128)(2,1)S(1)}, bf16[3,256,256]{2,1,0:T(8,128)(2,1)S(1)}, bf16[16,16,256]{2,1,0:T(8,128)(2,1)S(1)}, bf16[32,8,256]{2,1,...) custom-call(s32[1,1,16]{2,1,0:T(1,128)} %ids_hbm.3, ...), custom_call_target="tpu_custom_call" | custom-call | tf_op jit(solution)/shard_map/exchange/pallas_call | solution.py:468
  41.7 4.1 %finish.1 = bf16[1,1,16,256,256]{4,3,2,1,0:T(8,128)(2,1)} custom-call(s32[1,1,16]{2,1,0:T(1,128)} %ids_hbm.3, s32[1,1]{1,0:T(1,128)S(6)} %copy.7.counts, bf16[3,256,256]{2,1,0:T(8,128)(2,1)S(1)} %get-tuple-element.13.hot, bf16[3,256,256]{2,1,0:T(8,128)(2,1)S(1)} %get-tuple-element.14.keep, bf16[7,256,256]{2,1,0:T(8,128)(2,1)S(1)} %get-tuple-element.15.both, ...), custom_call_target="tpu_custom_call" | custom-call | tf_op jit(solution)/shard_map/finish/pallas_call | solution.py:489
